TPU v7x, 256 devices: a whole 4x4x8 slice. The times are simulated.
256 devices in a mesh: tensor: 64 (over x_hi, y, z), dp: 4 (over x_lo, core).
Axes of the slice: x: 4 (x_hi: 2, x_lo: 2; x = x_hi * 2 + x_lo), y: 4, z: 8, core: 2. Of those that a mesh axis runs over, the one named last changes fastest.
Arguments:
- base_weight: bfloat16 [2, 2, 4096, 14336], P(None, None, 'tensor', 'dp'), may hold values from -0.25 to 0.25
- adapter_left: bfloat16 [2, 2, 4096, 16], P(None, None, 'tensor'), may hold values from -0.059814453 to 0.059814453
- adapter_right: bfloat16 [2, 2, 16, 14336], P(None, None, None, 'dp'), may hold values from -1.5 to 1.5
- magnitude: bfloat16 [2, 2, 14336], P(None, None, 'dp'), may hold values from 16 to 256
Outputs:
- merged_weight: bfloat16 [2, 2, 14336, 4096], P(None, None, 'tensor')
All inputs are finite; a program needn't handle non-finite values.
Results may differ from a plain program's by a relative error of at most 0.0004.
Values may be sent and summed in bfloat16 or wider, within the bound.
A program may use at most 128 MiB of HBM per device.

v0:
```python
import jax
import jax.numpy as jnp
from jax import lax
from jax.sharding import PartitionSpec as P


def cut_along(array, dim, length):
    before, after = (array.shape[:dim], array.shape[dim + 1 :])
    return jnp.moveaxis(array.reshape(*before, length, -1, *after), dim, 0)


def edges_of(length, count):
    lap = length // count
    if lap >= 8:
        lap -= lap % 8
    return [lap * k for k in range(1, count)]


def laid_out(tiles, dim):
    tiles = jnp.moveaxis(tiles, 0, dim)
    shape = tiles.shape
    return tiles.reshape(*shape[:dim], shape[dim] * shape[dim + 1], *shape[dim + 2 :])


def exchange_in_pieces(array, axis, pieces, split_dim, concat_dim):
    tiles = cut_along(array, split_dim, lax.axis_size(axis))
    split_at = max(range(1, max(2, tiles.ndim - 1)), key=lambda d: tiles.shape[d])
    finished = []
    for piece in jnp.split(tiles, edges_of(tiles.shape[split_at], pieces), axis=split_at):
        if piece.size:
            finished.append(lax.all_to_all(piece, axis, split_axis=0, concat_axis=0, tiled=True))
    return laid_out(jnp.concatenate(finished, axis=split_at), concat_dim)


def copy_for_each(array, axis):
    copies = jnp.broadcast_to(array, (lax.axis_size(axis), *array.shape))
    return lax.all_to_all(copies, axis, split_axis=0, concat_axis=0, tiled=True)


def collect(array, axis, dim):
    tiles = copy_for_each(array, axis)
    return laid_out(tiles, dim)


def turned_gather(arrays, axis, dims):
    turned = [jnp.moveaxis(a, dim, 0) for a, dim in zip(arrays, dims)]
    widths = [t[0].size for t in turned]
    both = jnp.concatenate([t.reshape(-1, w) for t, w in zip(turned, widths)], axis=1)
    whole = lax.all_gather(both, axis, axis=0, tiled=True)
    tiles = jnp.split(whole, [sum(widths[:k]) for k in range(1, len(widths))], axis=1)
    return tuple(
        (
            jnp.moveaxis(b.reshape(-1, *t.shape[1:]), 0, dim)
            for b, t, dim in zip(tiles, turned, dims)
        )
    )


def regroup(weight_slab):
    experts, projections, row_count, col_count = weight_slab.shape
    tensor_count = lax.axis_size("tensor")
    replica_count = lax.axis_size("dp")
    serve_cols = col_count * replica_count // tensor_count
    quartered = lax.all_to_all(weight_slab, "dp", split_axis=2, concat_axis=3, tiled=True)
    grouped = exchange_in_pieces(quartered, "tensor", 2, 3, 2)
    collected = lax.all_gather(grouped, "dp", axis=2, tiled=True)
    pieces_view = collected.reshape(
        experts, projections, replica_count, tensor_count, row_count // replica_count, serve_cols
    )
    return pieces_view.transpose(0, 1, 5, 3, 2, 4).reshape(
        experts, projections, serve_cols, tensor_count * row_count
    )


def shards(base_weight, adapter_left, adapter_right, magnitude):
    tensor_count = lax.axis_size("tensor")
    replica_count = lax.axis_size("dp")
    col_count = base_weight.shape[3]
    serve_cols = col_count * replica_count // tensor_count
    arrived = regroup(base_weight)
    left_full = collect(adapter_left, "tensor", 2)
    right_all, magnitude_all = turned_gather((adapter_right, magnitude), "dp", (3, 2))
    col_start = lax.axis_index("tensor") * serve_cols
    right_cols = lax.dynamic_slice_in_dim(right_all, col_start, serve_cols, 3)
    magnitude_cols = lax.dynamic_slice_in_dim(magnitude_all, col_start, serve_cols, 2)
    merged = arrived.astype(jnp.float32) + jnp.einsum(
        "xyrf,xyir->xyfi", right_cols, left_full, preferred_element_type=jnp.float32
    )
    squares = jnp.sum(merged * merged, axis=3)
    scaling = magnitude_cols.astype(jnp.float32) / jnp.sqrt(squares + 1e-06)
    return (merged * scaling[:, :, :, None]).astype(jnp.bfloat16)


def solution(mesh):
    in_specs = (
        P(None, None, "tensor", "dp"),
        P(None, None, "tensor", None),
        P(None, None, None, "dp"),
        P(None, None, "dp"),
    )
    out_specs = P(None, None, "tensor", None)
    return jax.shard_map(shards, mesh=mesh, in_specs=in_specs, out_specs=out_specs, check_vma=False)
```

profile of v0, /device:TPU:1, one launch (start us, length us, event | category | flops | bytes accessed | tf_op | source)
XLA Modules:
  0.0 277.2 jit_solution(4250908606678984291)
XLA Ops:
  6.5 0.0 copy-start
  6.5 3.4 %copy.9 = bf16[2,2,64,3584]{3,1,0,2:T(2,128)(2,1)S(1)} copy(bf16[2,2,64,3584]{3,2,1,0:T(8,128)(2,1)} %param.4) | data formatting | bytes 3670016 | tf_op args[0]
  9.9 27.5 %all_to_all.30 = bf16[2,2,64,3584]{3,1,0,2:T(2,128)(2,1)S(1)} all-to-all(bf16[2,2,64,3584]{3,1,0,2:T(2,128)(2,1)S(1)} %copy.9), channel_id=1, replica_groups=mesh['tensor'=64,'dp'=4] {'dp'}, dimensions={2} | all-to-all | bytes 3670016 | tf_op jit(solution)/shard_map/all_to_all | solution.py:64
  37.4 2.6 copy.18
  40.1 4.4 %reshape.29 = bf16[2,2,16,64,224]{4,3,2,1,0:T(8,128)(2,1)S(1)} reshape(bf16[2,2,16,4,3584]{4,3,2,1,0:T(4,128)(2,1)} %bitcast.45) | data formatting | bytes 3670016 | tf_op jit(solution)/shard_map/reshape | solution.py:9
  44.5 0.0 copy-start.3
  44.5 0.2 fusion.3
  44.7 0.0 copy-start.2
  44.7 1.6 copy.12
  46.2 12.6 %all-to-all-start.2 = ((bf16[64,2,2,8,224]{4,3,2,1,0:T(8,128)(2,1)}), bf16[64,2,2,8,224]{4,3,2,1,0:T(8,128)(2,1)S(1)}, u32[]{:S(2)}, u32[]{:S(2)}) async-start(bf16[64,2,2,8,224]{4,3,2,1,0:T(8,128)(2,1)} %copy.12), calls=%async_computation.2 | async-start | bytes 2097152 | tf_op jit(solution)/shard_map/all_to_all | solution.py:31
  58.8 0.0 all-gather.5.cloned.1.call-start
  58.9 0.0 copy-done.3
  58.9 0.0 copy-done.2
  58.9 0.9 pad_maximum_fusion
  59.8 0.0 all-gather.5.cloned.1.call-update
  59.8 0.0 all-gather.3.cloned.1.call-start
  59.8 0.6 copy.11
  60.4 26.0 %all-to-all-done.2 = bf16[64,2,2,8,224]{4,3,2,1,0:T(8,128)(2,1)S(1)} async-done(((bf16[64,2,2,8,224]{4,3,2,1,0:T(8,128)(2,1)}), bf16[64,2,2,8,224]{4,3,2,1,0:T(8,128)(2,1)S(1)}, u32[]{:S(2)}, u32[]{:S(2)}) %all-to-all-start.2) | async-done | bytes 917536 | tf_op jit(solution)/shard_map/all_to_all | solution.py:31
  86.4 34.1 %all_to_all.31 = bf16[64,2,2,8,224]{4,3,2,1,0:T(8,128)(2,1)S(1)} all-to-all(bf16[64,2,2,8,224]{4,3,2,1,0:T(8,128)(2,1)S(1)} %copy.11), channel_id=1, replica_groups=mesh['tensor'=64,'dp'=4] {'tensor'}, dimensions={0} | all-to-all | bytes 1835008 | tf_op jit(solution)/shard_map/all_to_all | solution.py:31
  120.5 0.6 maximum_bitcast_fusion
  121.1 1.5 copy.13
  122.6 0.0 all-gather.3.cloned.1.call-update
  122.6 0.0 copy-done
  122.7 0.2 broadcast_bitcast_fusion
  122.9 1.6 reshape.38
  124.5 8.6 %all-to-all-start.3 = ((bf16[64,2,2048]{2,1,0:T(2,128)(2,1)}), bf16[64,2,2048]{2,1,0:T(2,128)(2,1)S(1)}, u32[]{:S(2)}, u32[]{:S(2)}) async-start(bf16[64,2,2048]{2,1,0:T(2,128)(2,1)} %reshape.38), calls=%async_computation.3 | async-start | bytes 1048576 | tf_op jit(solution)/shard_map/all_to_all | solution.py:37
  133.1 15.9 %all-to-all-done.3 = bf16[64,2,2048]{2,1,0:T(2,128)(2,1)S(1)} async-done(((bf16[64,2,2048]{2,1,0:T(2,128)(2,1)}), bf16[64,2,2048]{2,1,0:T(2,128)(2,1)S(1)}, u32[]{:S(2)}, u32[]{:S(2)}) %all-to-all-start.3) | async-done | bytes 524320 | tf_op jit(solution)/shard_map/all_to_all | solution.py:37
  149.0 0.7 reshape.39
  149.6 0.1 bitcast_bitcast_fusion
  149.8 0.7 copy.15
  150.5 0.8 reshape.34
  151.3 0.0 all-gather.5.cloned.1.call-done
  151.3 1.0 split.19
  152.3 0.1 reshape.35
  152.4 57.5 %all-gather.3.cloned.1.call-done = bf16[2,2,4096,224]{3,2,1,0:T(8,128)(2,1)} async-done(((bf16[2,2,1024,224]{3,2,1,0:T(8,128)(2,1)}), bf16[2,2,4096,224]{3,2,1,0:T(8,128)(2,1)}) %all-gather.3.cloned.1.call-update) | async-done | bytes 7340048 | tf_op jit(solution)/shard_map/all_gather | solution.py:66
  209.9 11.4 %convert_bitcast_fusion = f32[2,2,224,64,4,16]{2,5,3,4,1,0:T(8,128)} fusion(bf16[2,2,4,64,16,224]{5,4,3,2,1,0:T(8,128)(2,1)} %bitcast.41), kind=kLoop, calls=%fused_computation | loop fusion | flops 3670016 | bytes 22020096 | tf_op jit(solution)/shard_map/convert_element_type | solution.py:86
  221.3 11.9 %copy.14 = f32[2,2,224,64,4,16]{2,5,4,3,1,0:T(8,128)} copy(f32[2,2,224,64,4,16]{2,5,3,4,1,0:T(8,128)} %convert_bitcast_fusion) | data formatting | bytes 29360128 | tf_op jit(solution)/shard_map/convert_element_type | solution.py:86
  233.2 0.0 slice-start
  233.2 17.0 %copy.16 = f32[2,2,224,4096]{3,2,1,0:T(8,128)} copy(f32[2,2,224,4096]{2,3,1,0:T(8,128)} %bitcast.40) | data formatting | bytes 29360128 | tf_op jit(solution)/shard_map/convert_element_type | solution.py:86
  250.2 0.0 slice-done
  250.2 9.5 %multiply_reduce_fusion = (f32[2,2,224]{2,1,0:T(2,128)S(1)}, f32[2,2,224,4096]{3,2,1,0:T(8,128)}) fusion(f32[2,2,224,4096]{3,2,1,0:T(8,128)} %copy.16, bf16[2,2,4096,16]{2,3,1,0:T(8,128)(2,1)S(1)} %reshape.34, bf16[14336,2,2,16]{0,3,2,1:T(8,128)(2,1)S(1)} %bitcast.46, s32[]{:T(128)S(6)} %select_n.4), kind=kOutput, calls=%fused_computation.2 | convolution fusion | flops 128449664 | bytes 29920772 | tf_op jit(solution)/shard_map/xyrf,xyir->xyfi/dot_general | solution.py:86
  259.7 0.1 bitcast_multiply_fusion
  259.8 0.0 copy-start.1
  259.8 10.6 %multiply_convert_fusion = bf16[2,2,224,4096]{3,2,1,0:T(8,128)(2,1)} fusion(f32[2,2,224,4096]{3,2,1,0:T(8,128)} %get-tuple-element.8, f32[2,2,224]{2,1,0:T(2,128)S(1)} %bitcast_multiply_fusion), kind=kLoop, calls=%fused_computation.1 | loop fusion | flops 7340032 | bytes 22023680 | tf_op jit(solution)/shard_map/convert_element_type | solution.py:91
  270.4 0.0 copy-done.1
  (1 shorter events, 0.0 us)
Async XLA Ops:
  6.5 116.1 %copy-start = (bf16[2,2,64,16]{2,3,1,0:T(8,128)(2,1)S(1)}, bf16[2,2,64,16]{2,3,1,0:T(8,128)(2,1)}, u32[]{:S(2)}) copy-start(bf16[2,2,64,16]{2,3,1,0:T(8,128)(2,1)} %param.5) | copy-start | bytes 24580
  44.5 14.4 %copy-start.3 = (bf16[2,2,3584]{2,1,0:T(2,128)(2,1)S(1)}, bf16[2,2,3584]{2,1,0:T(2,128)(2,1)}, u32[]{:S(2)}) copy-start(bf16[2,2,3584]{2,1,0:T(2,128)(2,1)} %param.7) | copy-start | bytes 86020
  44.7 14.2 %copy-start.2 = (bf16[2,2,16,3584]{3,2,1,0:T(8,128)(2,1)S(1)}, bf16[2,2,16,3584]{3,2,1,0:T(8,128)(2,1)}, u32[]{:S(2)}) copy-start(bf16[2,2,16,3584]{3,2,1,0:T(8,128)(2,1)} %param.6) | copy-start | bytes 1376260
  46.2 40.2 %all-to-all-start.2 = ((bf16[64,2,2,8,224]{4,3,2,1,0:T(8,128)(2,1)}), bf16[64,2,2,8,224]{4,3,2,1,0:T(8,128)(2,1)S(1)}, u32[]{:S(2)}, u32[]{:S(2)}) async-start(bf16[64,2,2,8,224]{4,3,2,1,0:T(8,128)(2,1)} %copy.12), calls=%async_computation.2 | async-start | bytes 2097152 | tf_op jit(solution)/shard_map/all_to_all | solution.py:31
  58.8 92.5 %all-gather.5.cloned.1.call-start = ((), (), s32[]{:S(2)}) async-start(), calls=%async_computation.5 | async-start | bytes 2580480 | tf_op jit(solution)/shard_map/all_gather | solution.py:49
  59.8 150.1 %all-gather.3.cloned.1.call-start = ((), (), s32[]{:S(2)}) async-start(), calls=%async_computation.4 | async-start | bytes 10485760 | tf_op jit(solution)/shard_map/all_gather | solution.py:66
  124.5 24.5 %all-to-all-start.3 = ((bf16[64,2,2048]{2,1,0:T(2,128)(2,1)}), bf16[64,2,2048]{2,1,0:T(2,128)(2,1)S(1)}, u32[]{:S(2)}, u32[]{:S(2)}) async-start(bf16[64,2,2048]{2,1,0:T(2,128)(2,1)} %reshape.38), calls=%async_computation.3 | async-start | bytes 1048576 | tf_op jit(solution)/shard_map/all_to_all | solution.py:37
  233.2 17.0 %slice-start = ((bf16[14336,68]{0,1:T(8,128)(2,1)}), bf16[14336,64]{0,1:T(8,128)(2,1)S(1)}, s32[]{:S(2)}) async-start(bf16[14336,68]{0,1:T(8,128)(2,1)} %all-gather.5.cloned.1.call-done), calls=%async_computation.6 | async-start | bytes 3670016 | tf_op jit(solution)/shard_map/split | solution.py:50
  259.8 10.6 %copy-start.1 = (bf16[2,2,64,16]{2,3,1,0:T(8,128)(2,1)S(1)}, bf16[2,2,64,16]{2,3,1,0:T(8,128)(2,1)}, u32[]{:S(2)}) copy-start(bf16[2,2,64,16]{2,3,1,0:T(8,128)(2,1)} %param.5) | copy-start | bytes 24580
Sparse Core Ops, SparseCore 0:
  61.4 38.3 all-gather.4
  122.8 87.0 all-gather.2
where the time goes:
time: 278 us; the launch traced here: 277 us
  waiting for transfers between devices  99.4 us (36%)
  blocking collectives  61.6 us (22%)
  local copies, waits for them, and re-layouts  48.4 us (17%)
  other arithmetic  23.6 us (8%)
  starting transfers between devices  21.3 us (8%)
  between operations  13.6 us (5%)
  matrix products  9.51 us (3%)
    all_gather x1, waiting for transfers between devices, regroup(): collected = lax.all_gather(grouped, 'dp', axis=2, tiled=True)  57.5 us
    all_to_all x1, blocking collectives, exchange_in_pieces(): lax.all_to_all(piece, axis, split_axis=0, concat_axis=0, tiled=True)  34.1 us
    convert_element_type x2, local copies, waits for them, and re-layouts, shards(): arrived.astype(jnp.float32)  28.9 us
    all_to_all x1, blocking collectives, regroup(): lax.all_to_all(weight_slab, 'dp', split_axis=2, concat_axis=3, tiled=True)  27.5 us
    all_to_all x1, waiting for transfers between devices, exchange_in_pieces(): lax.all_to_all(piece, axis, split_axis=0, concat_axis=0, tiled=True)  26 us
    all_to_all x1, waiting for transfers between devices, copy_for_each(): return lax.all_to_all(copies, axis, split_axis=0, concat_axis=0, tiled=True)  15.9 us
    all_to_all x1, starting transfers between devices, exchange_in_pieces(): lax.all_to_all(piece, axis, split_axis=0, concat_axis=0, tiled=True)  12.6 us
    convert_element_type x1, other arithmetic, shards(): arrived.astype(jnp.float32)  11.4 us
  transfers between devices with their start and end apart: 4, of which 3 were waited for; matrix products, arithmetic and copies ran while one was open for 3% of the time, Pallas kernels for 0%

commit v1 on v0

v1 whole, which is shorter than its diff:
```python
import functools

import jax
import jax.numpy as jnp
from jax import lax
from jax.experimental import pallas as pl
from jax.experimental.pallas import tpu as pltpu
from jax.sharding import PartitionSpec as P

MESH = pl.DeviceIdType.MESH
F32, BF16 = jnp.float32, jnp.bfloat16

T = 64
ROWS = 64
SERVE = 224
EPS = 4
TILES = 7
WROWS = TILES * ROWS
LROWS = 32
BROWS = WROWS + LROWS
RROWS = 32

DZ_EVEN = (4, 2, -2, 0)
DZ_ODD = (-3, -1, 3, 1)
DZ_SEND = (4, -3, 2, -1, -2, 3, 1, 0)


def packed(load, m):
    hole = 3 - m
    full = [load(e, 2 * m) for e in range(EPS)]
    rest = []
    for e in range(EPS):
        if m == 0:
            rest.append(load(e, 1))
        elif m == 3:
            rest.append(load(e, 5))
        else:
            low, high = load(e, 2 * m + 1), load(e, 2 * m - 1)
            group = lax.broadcasted_iota(jnp.int32, low.shape, 1) // 32
            rest.append(jnp.where(group < hole, low, high))
    last = rest[3]
    group = lax.broadcasted_iota(jnp.int32, last.shape, 1) // 32
    for k in range(3):
        full.append(jnp.where(group == hole, pltpu.roll(last, 32 * (k + 1), 1), rest[k]))
    return full


def comm_kernel(x_ref, l_ref, r_ref, m_ref, recv_ref, rm_ref, send_buf, rsend, a_send, f_send, r_send, recv_sem, r_recv):
    t, q = lax.axis_index("tensor"), lax.axis_index("dp")
    xh, y, z = t // 32, (t // 8) % 4, t % 8
    xl, c = q // 2, q % 2
    nbr, peer = q + 2 - 4 * xl, q + 1 - 2 * c

    src_q = xh * 2 + y // 2

    def direct(s):
        i, p, h = s // 4, (s // 2) % 2, s % 2
        odd = (z + c) % 2
        dz = jnp.where(odd == 1, DZ_ODD[i], DZ_EVEN[i])
        zs = (z - dz + 8) % 8
        ys = (y + p) % 2 + 2 * h
        return ys * 8 + zs

    barrier = pltpu.get_barrier_semaphore()
    self_in = 0
    for s in range(16):
        ts = xl * 32 + direct(s)
        same = jnp.logical_and(ts == t, src_q == q)
        self_in = self_in + same.astype(jnp.int32)

        @pl.when(jnp.logical_not(same))
        def _():
            pl.semaphore_signal(barrier, inc=1, device_id=(ts, src_q), device_id_type=MESH)

    for other in (nbr, peer, 3 - q):
        pl.semaphore_signal(barrier, inc=1, device_id=(t, other), device_id_type=MESH)

    lanes = lax.broadcasted_iota(jnp.int32, (16, 128), 1)
    ranks = lax.broadcasted_iota(jnp.int32, (16, 128), 0)
    lpack = jnp.zeros((LROWS, 128), F32)
    for half in range(2):
        for e in range(EPS):
            place = (lanes == half * 64 + e * 16 + ranks).astype(BF16)
            lpack += jnp.dot(l_ref[e, half * 32 : half * 32 + 32, :], place, preferred_element_type=F32)
    lpack = lpack.astype(BF16)

    @pl.loop(0, 4)
    def _(g):
        base = g * (TILES * 128)

        def at(k):
            return pl.ds(pl.multiple_of(base + 128 * k, 128), 128)

        for m in range(4):
            d = g * 4 + m
            for j, tile in enumerate(packed(lambda e, k: x_ref[e, :, at(k)].astype(F32), m)):
                send_buf[d, j * ROWS : (j + 1) * ROWS, :] = tile.astype(BF16)
            send_buf[d, WROWS:, :] = lpack
            rt = packed(lambda e, k: r_ref[e, :, at(k)].astype(F32), m)
            mt = packed(lambda e, k: m_ref[:, at(k)].astype(F32)[e : e + 1], m)
            for j in range(TILES):
                rows = jnp.concatenate([rt[j], jnp.broadcast_to(mt[j], (16, 128))], axis=0)
                rsend[d, j * RROWS : (j + 1) * RROWS, :] = rows.astype(BF16)

    self_out = jnp.logical_and(jnp.logical_and(xl == xh, y // 2 == c), z % 2 == c).astype(jnp.int32)
    pl.semaphore_wait(barrier, 19 - self_out)
    dst_q = xh * 2 + z % 2

    def block_copy(src, slot, send, dev):
        return pltpu.make_async_remote_copy(
            src_ref=src, dst_ref=recv_ref.at[slot], send_sem=send, recv_sem=recv_sem.at[slot], device_id=dev, device_id_type=MESH
        )

    def outgoing(k):
        dz, p = DZ_SEND[k // 2], k % 2
        yd, zd = (y + p) % 2, (z + dz + 8) % 8
        d = yd * 8 + zd
        td = 16 * q + d
        same = jnp.logical_and(td == t, dst_q == q)
        return d, td, same

    for k in range(16):
        d, td, same = outgoing(k)

        @pl.when(same)
        def _():
            pltpu.make_async_copy(send_buf.at[d], recv_ref.at[t], recv_sem.at[t]).start()

        @pl.when(jnp.logical_not(same))
        def _():
            block_copy(send_buf.at[d], t, a_send.at[k], (td, dst_q)).start()

    owner = t // 16
    mine = q == owner

    def r_copy(k):
        return pltpu.make_async_remote_copy(
            src_ref=rsend.at[t % 16], dst_ref=rm_ref, send_sem=r_send.at[k], recv_sem=r_recv, device_id=(t, (q + 1 + k) % 4), device_id_type=MESH
        )

    @pl.when(mine)
    def _():
        for k in range(3):
            r_copy(k).start()
        pltpu.make_async_copy(rsend.at[t % 16], rm_ref, r_recv).start()

    def arrived(slot):
        block_copy(recv_ref.at[slot], slot, f_send.at[0], (t, peer)).wait_recv()

    def forward(slot, k, other):
        block_copy(recv_ref.at[slot], slot, f_send.at[k], (t, other)).start()

    for s in range(17):
        if s < 16:
            slot = xl * 32 + direct(s)
            arrived(slot)
            forward(slot, s, nbr)
            forward(slot, 16 + s, peer)
        if s >= 1:
            slot = (1 - xl) * 32 + direct(s - 1)
            arrived(slot)
            forward(slot, 32 + s - 1, peer)

    @pl.loop(0, 32)
    def _(n):
        arrived(n * 2 + 1 - c)

    pltpu.make_async_copy(rsend.at[0], rm_ref, r_recv).wait()
    for k in range(16):
        d, td, same = outgoing(k)

        @pl.when(jnp.logical_not(same))
        def _():
            block_copy(send_buf.at[d], t, a_send.at[k], (td, dst_q)).wait_send()

    @pl.loop(0, 48)
    def _(k):
        block_copy(recv_ref.at[0], 0, f_send.at[k], (t, peer)).wait_send()

    @pl.when(mine)
    def _():
        for k in range(3):
            r_copy(k).wait_send()


def nt(a, b):
    return lax.dot_general(a, b, (((1,), (1,)), ((), ())), preferred_element_type=F32)


def merge_kernel(w_ref, rm_ref, out_ref, merged, acc, lhs):
    m = lax.axis_index("tensor") % 4
    hole = 3 - m
    lane = lax.broadcasted_iota(jnp.int32, (128, 128), 1)
    row = lax.broadcasted_iota(jnp.int32, (128, 128), 0)
    eye = (lane == row).astype(BF16)

    mags = []
    for j in range(TILES):
        r = rm_ref[j * RROWS : j * RROWS + 16, :].astype(F32)
        r8 = jnp.concatenate([r] * 8, axis=0)
        e_row = (row // 16) % 4
        e_lane = j if j < 4 else jnp.where(lane // 32 == hole, 3, j - 4)
        rbd = jnp.where(e_row == e_lane, r8, 0.0).astype(BF16)
        lhs[j, :, 0:128] = eye
        lhs[j, :, 128:256] = nt(eye, rbd).astype(BF16)
        mags.append(nt(eye, rm_ref[j * RROWS + 16 : j * RROWS + 32, :])[:, 0:1])

    acc[...] = jnp.zeros_like(acc)
    low = lax.broadcasted_iota(jnp.int32, (LROWS, 128), 1) < 64

    @pl.loop(0, 16)
    def _(n):
        parts = []
        for k in range(4):
            lb = w_ref[n * 4 + k, WROWS:, :].astype(F32)
            parts += [jnp.where(low, lb, 0.0), jnp.where(low, 0.0, lb)]
        lm = jnp.concatenate(parts, axis=0).astype(BF16)
        for j in range(TILES):
            w = jnp.concatenate([w_ref[n * 4 + k, j * ROWS : (j + 1) * ROWS, :] for k in range(4)], axis=0)
            rhs = jnp.concatenate([w, lm], axis=1)
            o = nt(lhs[j], rhs)
            merged[j * 128 : (j + 1) * 128, pl.ds(pl.multiple_of(n * 256, 256), 256)] = o
            o2 = o * o
            acc[j * 128 : (j + 1) * 128, :] += o2[:, :128] + o2[:, 128:]

    def column(g):
        return jnp.where(g > hole, 32 * (g - hole - 1), 128 + 32 * m + 32 * g)

    for j in range(TILES):
        squares = jnp.sum(acc[j * 128 : (j + 1) * 128, :], axis=1, keepdims=True)
        scale = mags[j] / jnp.sqrt(squares + 1e-6)
        for g in range(4):
            if j < 4:
                start = SERVE * j + 32 * m + 32 * g
            else:
                k = j - 4
                from3 = (hole - k - 1 + 4) % 4
                start = jnp.where(hole == g, SERVE * 3 + column(from3), SERVE * k + column(g))
            rows = slice(j * 128 + g * 32, j * 128 + g * 32 + 32)
            out_ref[pl.ds(pl.multiple_of(start, 32), 32), :] = (merged[rows, :] * scale[g * 32 : g * 32 + 32]).astype(BF16)


def shards(base_weight, adapter_left, adapter_right, magnitude):
    x = base_weight.reshape(EPS, ROWS, 3584)
    left = adapter_left.reshape(EPS, ROWS, 16)
    right = adapter_right.reshape(EPS, 16, 3584)
    mag = magnitude.reshape(EPS, 3584)
    vmem = pl.BlockSpec(memory_space=pltpu.VMEM)
    recv, rm = pl.pallas_call(
        comm_kernel,
        out_shape=(jax.ShapeDtypeStruct((T, BROWS, 128), BF16), jax.ShapeDtypeStruct((TILES * RROWS, 128), BF16)),
        in_specs=[vmem] * 4,
        out_specs=(vmem, vmem),
        scratch_shapes=[
            pltpu.VMEM((16, BROWS, 128), BF16),
            pltpu.VMEM((16, TILES * RROWS, 128), BF16),
            pltpu.SemaphoreType.DMA((16,)),
            pltpu.SemaphoreType.DMA((48,)),
            pltpu.SemaphoreType.DMA((3,)),
            pltpu.SemaphoreType.DMA((T,)),
            pltpu.SemaphoreType.DMA,
        ],
        compiler_params=pltpu.CompilerParams(collective_id=0, has_side_effects=True),
        name="exchange",
    )(x, left, right, mag)
    out = pl.pallas_call(
        merge_kernel,
        out_shape=jax.ShapeDtypeStruct((EPS * SERVE, T * ROWS), BF16),
        in_specs=[vmem] * 2,
        out_specs=vmem,
        scratch_shapes=[
            pltpu.VMEM((EPS * SERVE, T * ROWS), F32),
            pltpu.VMEM((EPS * SERVE, 128), F32),
            pltpu.VMEM((TILES, 128, 256), BF16),
        ],
        compiler_params=pltpu.CompilerParams(vmem_limit_bytes=60 * 2**20),
        name="merge",
    )(recv, rm)
    return out.reshape(2, 2, SERVE, T * ROWS)


def solution(mesh):
    in_specs = (
        P(None, None, "tensor", "dp"),
        P(None, None, "tensor", None),
        P(None, None, None, "dp"),
        P(None, None, "dp"),
    )
    out_specs = P(None, None, "tensor", None)
    return jax.shard_map(shards, mesh=mesh, in_specs=in_specs, out_specs=out_specs, check_vma=False)
```

time: 278 us -> 106 us (0.38)
  Pallas kernels: 0 us -> 103 us
  waiting for transfers between devices: 99.4 us -> 0 us
  blocking collectives: 61.6 us -> 0 us
  local copies, waits for them, and re-layouts: 48.4 us -> 2.8 us
  other arithmetic: 23.6 us -> 0 us
  starting transfers between devices: 21.3 us -> 0 us
  between operations: 13.6 us -> 0.01 us
  matrix products: 9.51 us -> 0 us
    pallas_call x0 -> x2, Pallas kernels: none -> 103 us  [the longest x1 87 us: shards(): pl.pallas_call(comm_kernel, out_shape=(jax.ShapeDtypeStruct((T, BROWS, 12...]
    all_to_all x2 -> x0, blocking collectives: 61.6 us -> none  [the longest x1 34.1 us: exchange_in_pieces(): lax.all_to_all(piece, axis, split_axis=0, concat_axis=0, tiled=True)]
    all_gather x2 -> x0, waiting for transfers between devices: 57.6 us -> none  [the longest x1 57.5 us: regroup(): collected = lax.all_gather(grouped, 'dp', axis=2, tiled=True)]
    all_to_all x2 -> x0, waiting for transfers between devices: 41.8 us -> none  [the longest x1 26 us: exchange_in_pieces(): lax.all_to_all(piece, axis, split_axis=0, concat_axis=0, tiled=True)]
    convert_element_type x2 -> x0, local copies, waits for them, and re-layouts: 28.9 us -> none  [shards(): arrived.astype(jnp.float32)]
    convert_element_type x2 -> x0, other arithmetic: 22 us -> none  [the longest x1 11.4 us: shards(): arrived.astype(jnp.float32)]
    all_to_all x2 -> x0, starting transfers between devices: 21.2 us -> none  [the longest x1 12.6 us: exchange_in_pieces(): lax.all_to_all(piece, axis, split_axis=0, concat_axis=0, tiled=True)]
    dot_general x1 -> x0, matrix products: 9.51 us -> none  [shards(): jnp.einsum('xyrf,xyir->xyfi', right_cols, left_full, preferred_element_ty...]
  transfers between devices with their start and end apart: 4 -> 0, of which waited for: 3 -> 0; matrix products, arithmetic and copies ran while one was open for 3% -> 0% of each run, Pallas kernels for 0% -> 0%
where the time goes in v1:
time: 106 us; the launch traced here: 105 us
  Pallas kernels  103 us (97%)
  local copies, waits for them, and re-layouts  2.8 us (3%)
    pallas_call x1, Pallas kernels, shards(): pl.pallas_call(comm_kernel, out_shape=(jax.ShapeDtypeStruct((T, BROWS, 12...  87 us
    pallas_call x1, Pallas kernels, shards(): pl.pallas_call(merge_kernel, out_shape=jax.ShapeDtypeStruct((EPS * SERVE,...  15.5 us

profile of v1, /device:TPU:1, one launch (start us, length us, event | category | flops | bytes accessed | tf_op | source)
XLA Modules:
  0.0 105.3 jit_solution(16342759580034946872)
XLA Ops:
  0.0 1.4 %reshape.18.m_ref = bf16[4,3584]{1,0:T(4,128)(2,1)} reshape(bf16[2,2,3584]{2,1,0:T(2,128)(2,1)} %param.7) | data formatting | bytes 57344 | tf_op jit(solution)/shard_map/reshape | solution.py:247
  1.4 1.4 %copy.5 = bf16[2,2,64,16]{3,2,1,0:T(8,128)(2,1)} copy(bf16[2,2,64,16]{2,3,1,0:T(8,128)(2,1)} %param.5) | data formatting | bytes 16384 | tf_op args[1]
  2.8 87.0 %exchange.1 = (bf16[64,480,128]{2,1,0:T(8,128)(2,1)}, bf16[224,128]{1,0:T(8,128)(2,1)}) custom-call(bf16[4,64,3584]{2,1,0:T(8,128)(2,1)} %bitcast.4, bf16[4,64,16]{2,1,0:T(8,128)(2,1)} %bitcast.6, bf16[4,16,3584]{2,1,0:T(8,128)(2,1)} %bitcast.5, bf16[4,3584]{1,0:T(4,128)(2,1)} %reshape.18.m_ref), custom_call_target="tpu_custom_call" | custom-call | tf_op jit(solution)/shard_map/exchange/pallas_call | solution.py:249
  89.8 15.5 %merge.1 = bf16[896,4096]{1,0:T(8,128)(2,1)} custom-call(bf16[64,480,128]{2,1,0:T(8,128)(2,1)} %get-tuple-element.7.w_ref, bf16[224,128]{1,0:T(8,128)(2,1)} %get-tuple-element.8.rm_ref), custom_call_target="tpu_custom_call" | custom-call | tf_op jit(solution)/shard_map/merge/pallas_call | solution.py:266

commit v2 on v1

v2 whole, which is shorter than its diff:
```python
import functools

import jax
import jax.numpy as jnp
from jax import lax
from jax.experimental import pallas as pl
from jax.experimental.pallas import tpu as pltpu
from jax.sharding import PartitionSpec as P

MESH = pl.DeviceIdType.MESH
F32, BF16 = jnp.float32, jnp.bfloat16

T = 64
ROWS = 64
SERVE = 224
EPS = 4
TILES = 7
WROWS = TILES * ROWS
LROWS = 32
BROWS = WROWS + LROWS
RROWS = 32
LAG1, LAG2 = 2, 2


def packed(load, m):
    hole = 3 - m
    full = [load(e, 2 * m) for e in range(EPS)]
    rest = []
    for e in range(EPS):
        if m == 0:
            rest.append(load(e, 1))
        elif m == 3:
            rest.append(load(e, 5))
        else:
            low, high = load(e, 2 * m + 1), load(e, 2 * m - 1)
            group = lax.broadcasted_iota(jnp.int32, low.shape, 1) // 32
            rest.append(jnp.where(group < hole, low, high))
    last = rest[3]
    group = lax.broadcasted_iota(jnp.int32, last.shape, 1) // 32
    for k in range(3):
        full.append(jnp.where(group == hole, pltpu.roll(last, 32 * (k + 1), 1), rest[k]))
    return full


def nt(a, b):
    return lax.dot_general(a, b, (((1,), (1,)), ((), ())), preferred_element_type=F32)


def offset(i):
    far = (i + 1) // 2
    return jnp.where(i % 2 == 1, far, -far)


def exchange_kernel(
    x_ref, l_ref, r_ref, m_ref, merged, scale_ref, send_buf, rsend, recv, relay, rm, acc, lhs, a_send, l_send, f_send, r_send, recv_sem, l_recv, r_recv
):
    t, q = lax.axis_index("tensor"), lax.axis_index("dp")
    xh, y, z = t // 32, (t // 8) % 4, t % 8
    xl, c = q // 2, q % 2
    nbr, peer = q + 2 - 4 * xl, q + 1 - 2 * c
    edge, inner = xh == xl, xh != xl
    mirror = (xl * 32 + y * 8 + z, 2 * xh + c)
    src_core, dst_core = y // 2, y % 2
    row_m = t % 4
    hole = 3 - row_m

    def source(s, parity):
        return (parity + 2 * (s % 2)) * 8 + (z - offset(s // 2) + 8) % 8

    barrier = pltpu.get_barrier_semaphore()

    @pl.loop(0, 16)
    def _(s):
        yz = source(s, c)

        @pl.when(jnp.logical_or(yz != y * 8 + z, src_core != c))
        def _():
            pl.semaphore_signal(barrier, inc=1, device_id=(xh * 32 + yz, xl * 2 + src_core), device_id_type=MESH)

    for other in (nbr, peer, 3 - q):
        pl.semaphore_signal(barrier, inc=1, device_id=(t, other), device_id_type=MESH)

    @pl.when(inner)
    def _():
        pl.semaphore_signal(barrier, inc=1, device_id=mirror, device_id_type=MESH)

    lanes = lax.broadcasted_iota(jnp.int32, (16, 128), 1)
    ranks = lax.broadcasted_iota(jnp.int32, (16, 128), 0)
    lpack = jnp.zeros((LROWS, 128), F32)
    for e in range(EPS):
        low = (lanes == e * 16 + ranks).astype(BF16)
        high = (lanes == 64 + e * 16 + ranks).astype(BF16)
        tn = functools.partial(lax.dot_general, dimension_numbers=(((0,), (0,)), ((), ())), preferred_element_type=F32)
        lpack += tn(l_ref[e], low)[:LROWS] + tn(l_ref[e], high)[LROWS:]
    lpack = lpack.astype(BF16)

    @pl.loop(0, 4)
    def _(g):
        base = g * (TILES * 128)

        def at(k):
            return pl.ds(pl.multiple_of(base + 128 * k, 128), 128)

        for m in range(4):
            d = g * 4 + m
            for j, tile in enumerate(packed(lambda e, k: x_ref[e, :, at(k)].astype(F32), m)):
                send_buf[d, j * ROWS : (j + 1) * ROWS, :] = tile.astype(BF16)
            send_buf[d, WROWS:, :] = lpack
            rt = packed(lambda e, k: r_ref[e, :, at(k)].astype(F32), m)
            mt = packed(lambda e, k: m_ref[e // 2, :, at(k)].astype(F32)[e % 2 : e % 2 + 1], m)
            for j in range(TILES):
                rows = jnp.concatenate([rt[j], jnp.broadcast_to(mt[j], (16, 128))], axis=0)
                rsend[d, j * RROWS : (j + 1) * RROWS, :] = rows.astype(BF16)

    self_out = jnp.logical_and(src_core == c, dst_core == c).astype(jnp.int32)
    pl.semaphore_wait(barrier, 19 - self_out + inner.astype(jnp.int32))

    def copy(src, dst, send, recv_s, dev):
        return pltpu.make_async_remote_copy(
            src_ref=src, dst_ref=dst, send_sem=send, recv_sem=recv_s, device_id=dev, device_id_type=MESH
        )

    mine = q == t // 16

    def r_copy(k):
        return copy(rsend.at[t % 16], rm, r_send.at[k], r_recv, (t, (q + 1 + k) % 4))

    @pl.when(mine)
    def _():
        for k in range(3):
            r_copy(k).start()
        pltpu.make_async_copy(rsend.at[t % 16], rm, r_recv).start()

    def outgoing(k):
        yd, zd = 2 * c + (y + k % 2) % 2, (z + offset(k // 2) + 8) % 8
        away = jnp.logical_or(jnp.logical_or(yd != y, zd != z), dst_core != c)
        return yd, zd, away

    @pl.loop(0, 16)
    def _(k):
        yd, zd, away = outgoing(k)
        d = (yd - 2 * c) * 8 + zd
        s = 2 * (k // 2) + y // 2
        dev = (xh * 32 + yd * 8 + zd, xl * 2 + dst_core)
        block = send_buf.at[d]

        @pl.when(jnp.logical_and(away, edge))
        def _():
            copy(block, recv.at[t], a_send.at[k], recv_sem.at[t], dev).start()

        @pl.when(jnp.logical_and(away, inner))
        def _():
            copy(block, relay.at[s], a_send.at[k], l_recv.at[s], dev).start()

        @pl.when(jnp.logical_and(jnp.logical_not(away), edge))
        def _():
            pltpu.make_async_copy(block, recv.at[t], recv_sem.at[t]).start()

        @pl.when(jnp.logical_and(jnp.logical_not(away), inner))
        def _():
            pltpu.make_async_copy(block, relay.at[s], l_recv.at[s]).start()

    def arrived(slot):
        copy(recv.at[slot], recv.at[slot], f_send.at[0], recv_sem.at[slot], (t, peer)).wait_recv()

    def forward(slot, k, other):
        copy(recv.at[slot], recv.at[slot], f_send.at[k], recv_sem.at[slot], (t, other)).start()

    def relayed(s):
        slot = xh * 32 + source(s, c)
        return copy(relay.at[s], recv.at[slot], l_send.at[s], recv_sem.at[slot], mirror)

    lane = lax.broadcasted_iota(jnp.int32, (128, 128), 1)
    row = lax.broadcasted_iota(jnp.int32, (128, 128), 0)
    eye = (lane == row).astype(BF16)

    def build_lhs():
        pltpu.make_async_copy(rsend.at[0], rm, r_recv).wait()
        for j in range(TILES):
            r = rm[j * RROWS : j * RROWS + 16, :].astype(F32)
            r8 = jnp.concatenate([r] * 8, axis=0)
            e_lane = j if j < 4 else jnp.where(lane // 32 == hole, 3, j - 4)
            rbd = jnp.where((row // 16) % 4 == e_lane, r8, 0.0).astype(BF16)
            lhs[j, :, 0:128] = eye
            lhs[j, :, 128:256] = nt(eye, rbd).astype(BF16)

    def column(g):
        return jnp.where(g > hole, 32 * (g - hole - 1), 128 + 32 * row_m + 32 * g)

    def row_start(j, g):
        if j < 4:
            return pl.multiple_of(SERVE * j + 32 * row_m + 32 * g, 32)
        k = j - 4
        from3 = (hole - k - 1 + 4) % 4
        return pl.multiple_of(jnp.where(hole == g, SERVE * 3 + column(from3), SERVE * k + column(g)), 32)

    starts = [[row_start(j, g) for g in range(4)] for j in range(TILES)]
    low_half = lax.broadcasted_iota(jnp.int32, (LROWS, 128), 1) < 64

    def unit(w):
        stage, who = w // 4, w % 4
        half = jnp.where(who >= 2, 1 - xl, xl)
        parity = jnp.where(who % 2 == 1, 1 - c, c)
        odd = z % 2
        step = jnp.where(stage == 0, 0, jnp.where(stage == 1, -2, jnp.where(stage == 2, 2, 4)))
        zp = (z - odd + (1 - 2 * odd) * step + 8) % 8
        firsts = [half * 32 + (parity + 2 * h) * 8 + zp for h in range(2)]
        slots = [f + k for f in firsts for k in range(2)]
        parts = []
        for s in slots:
            lb = recv[s, WROWS:, :].astype(F32)
            parts += [jnp.where(low_half, lb, 0.0), jnp.where(low_half, 0.0, lb)]
        lm = jnp.concatenate(parts, axis=0).astype(BF16)
        for j in range(TILES):
            wt = jnp.concatenate([recv[s, j * ROWS : (j + 1) * ROWS, :] for s in slots], axis=0)
            o = nt(lhs[j], jnp.concatenate([wt, lm], axis=1))
            for h in range(2):
                cols = pl.ds(pl.multiple_of(firsts[h] * 64, 128), 128)
                if j < 4:
                    merged[pl.ds(starts[j][0], 128), cols] = o[:, 128 * h : 128 * h + 128]
                else:
                    for g in range(4):
                        merged[pl.ds(starts[j][g], 32), cols] = o[32 * g : 32 * g + 32, 128 * h : 128 * h + 128]
            o2 = o * o
            acc[j * 128 : (j + 1) * 128, :] += o2[:, :128] + o2[:, 128:]

    acc[...] = jnp.zeros_like(acc)

    @pl.loop(0, 21)
    def _(s):
        @pl.when(jnp.logical_and(s < 16, inner))
        def _():
            copy(relay.at[s], relay.at[s], l_send.at[0], l_recv.at[s], mirror).wait_recv()
            relayed(s).start()

        a = s - LAG1

        @pl.when(jnp.logical_and(a >= 0, a < 16))
        def _():
            slot = xl * 32 + source(a, c)
            arrived(slot)
            forward(slot, a, nbr)
            forward(slot, 16 + a, peer)

        b = s - LAG1 - LAG2

        @pl.when(jnp.logical_and(b >= 0, b < 16))
        def _():
            slot = (1 - xl) * 32 + source(b, c)
            arrived(slot)
            forward(slot, 32 + b, peer)

        @pl.when(jnp.logical_and(a >= 1, a < 17))
        def _():
            arrived(xl * 32 + source(a - 1, 1 - c))

        @pl.when(jnp.logical_and(b >= 1, b < 17))
        def _():
            arrived((1 - xl) * 32 + source(b - 1, 1 - c))

        @pl.when(s == 6)
        def _():
            build_lhs()

        @pl.when(s >= 7)
        def _():
            @pl.loop(0, jnp.where(jnp.logical_or(s == 17, s == 18), 2, 1))
            def _(v):
                unit(jnp.where(s <= 16, s - 7, jnp.where(s <= 18, s - 7 + 2 * v, s - 5)))

    for j in range(TILES):
        squares = jnp.sum(acc[j * 128 : (j + 1) * 128, :], axis=1, keepdims=True)
        mags = nt(eye, rm[j * RROWS + 16 : j * RROWS + 32, :])[:, 0:1]
        scale = jnp.broadcast_to(mags / jnp.sqrt(squares + 1e-6), (128, 128))
        for g in range(4):
            scale_ref[pl.ds(starts[j][g], 32), :] = scale[32 * g : 32 * g + 32]

    @pl.loop(0, 16)
    def _(k):
        @pl.when(outgoing(k)[2])
        def _():
            copy(send_buf.at[0], relay.at[0], a_send.at[k], l_recv.at[0], mirror).wait_send()

        @pl.when(inner)
        def _():
            relayed(k).wait_send()

    @pl.loop(0, 48)
    def _(k):
        copy(recv.at[0], recv.at[0], f_send.at[k], recv_sem.at[0], (t, peer)).wait_send()

    @pl.when(mine)
    def _():
        for k in range(3):
            r_copy(k).wait_send()


def scale_kernel(merged, scale, out_ref):
    rows = pl.ds(pl.multiple_of(pl.program_id(0) * 64, 64), 64)
    s = scale[rows, :]

    @pl.loop(0, T * ROWS // 512)
    def _(k):
        for n in range(4):
            cols = pl.ds(pl.multiple_of(k * 512 + n * 128, 128), 128)
            out_ref[:, cols] = (merged[rows, cols] * s).astype(BF16)


def shards(base_weight, adapter_left, adapter_right, magnitude):
    x = base_weight.reshape(EPS, ROWS, 3584)
    left = jnp.swapaxes(adapter_left, 2, 3).reshape(EPS, 16, ROWS)
    right = adapter_right.reshape(EPS, 16, 3584)
    vmem = pl.BlockSpec(memory_space=pltpu.VMEM)
    merged, scale = pl.pallas_call(
        exchange_kernel,
        out_shape=(pltpu.VMEM((EPS * SERVE, T * ROWS), F32), pltpu.VMEM((EPS * SERVE, 128), F32)),
        in_specs=[vmem] * 4,
        out_specs=(vmem, vmem),
        scratch_shapes=[
            pltpu.VMEM((16, BROWS, 128), BF16),
            pltpu.VMEM((16, TILES * RROWS, 128), BF16),
            pltpu.VMEM((T, BROWS, 128), BF16),
            pltpu.VMEM((16, BROWS, 128), BF16),
            pltpu.VMEM((TILES * RROWS, 128), BF16),
            pltpu.VMEM((EPS * SERVE, 128), F32),
            pltpu.VMEM((TILES, 128, 256), BF16),
            pltpu.SemaphoreType.DMA((16,)),
            pltpu.SemaphoreType.DMA((16,)),
            pltpu.SemaphoreType.DMA((48,)),
            pltpu.SemaphoreType.DMA((3,)),
            pltpu.SemaphoreType.DMA((T,)),
            pltpu.SemaphoreType.DMA((16,)),
            pltpu.SemaphoreType.DMA,
        ],
        compiler_params=pltpu.CompilerParams(collective_id=0, has_side_effects=True, vmem_limit_bytes=24 * 2**20),
        name="exchange",
    )(x, left, right, magnitude)
    out = pl.pallas_call(
        scale_kernel,
        out_shape=jax.ShapeDtypeStruct((EPS * SERVE, T * ROWS), BF16),
        grid=(EPS * SERVE // 64,),
        in_specs=[vmem, vmem],
        out_specs=pl.BlockSpec((64, T * ROWS), lambda i: (i, 0)),
        compiler_params=pltpu.CompilerParams(vmem_limit_bytes=16 * 2**20),
        name="scale",
    )(merged, scale)
    return out.reshape(2, 2, SERVE, T * ROWS)


def solution(mesh):
    in_specs = (
        P(None, None, "tensor", "dp"),
        P(None, None, "tensor", None),
        P(None, None, None, "dp"),
        P(None, None, "dp"),
    )
    out_specs = P(None, None, "tensor", None)
    return jax.shard_map(shards, mesh=mesh, in_specs=in_specs, out_specs=out_specs, check_vma=False)
```

time: 106 us -> 87.1 us (0.82)
  Pallas kernels: 103 us -> 81.9 us
  local copies, waits for them, and re-layouts: 2.8 us -> 3.98 us
    pallas_call x2, Pallas kernels: 103 us -> 81.9 us  [the longest x1 74.5 us: shards(): pl.pallas_call(exchange_kernel, out_shape=(pltpu.VMEM((EPS * SERVE, T * R...]
    unnamed x1 -> x8, local copies, waits for them, and re-layouts: 1.43 us -> 3.98 us
    reshape x1 -> x0, local copies, waits for them, and re-layouts: 1.37 us -> none  [shards(): mag = magnitude.reshape(EPS, 3584)]
where the time goes in v2:
time: 87.1 us; the launch traced here: 85.9 us
  Pallas kernels  81.9 us (94%)
  local copies, waits for them, and re-layouts  3.98 us (5%)
    pallas_call x1, Pallas kernels, shards(): pl.pallas_call(exchange_kernel, out_shape=(pltpu.VMEM((EPS * SERVE, T * R...  74.5 us
    pallas_call x1, Pallas kernels, shards(): pl.pallas_call(scale_kernel, out_shape=jax.ShapeDtypeStruct((EPS * SERVE,...  7.37 us
    unnamed x8, local copies, waits for them, and re-layouts  3.98 us

profile of v2, /device:TPU:1, one launch (start us, length us, event | category | flops | bytes accessed | tf_op | source)
XLA Modules:
  0.0 85.9 jit_solution(6085721744627458000)
XLA Ops:
  0.0 0.0 copy-start
  0.0 1.5 %copy-done = bf16[2,2,64,3584]{3,2,1,0:T(8,128)(2,1)S(1)} copy-done((bf16[2,2,64,3584]{3,2,1,0:T(8,128)(2,1)S(1)}, bf16[2,2,64,3584]{3,2,1,0:T(8,128)(2,1)}, u32[]{:S(2)}) %copy-start) | copy-done | bytes 1835032
  1.5 0.0 copy-start.1
  1.5 1.0 %copy-done.1 = bf16[2,2,16,3584]{3,2,1,0:T(8,128)(2,1)S(1)} copy-done((bf16[2,2,16,3584]{3,2,1,0:T(8,128)(2,1)S(1)}, bf16[2,2,16,3584]{3,2,1,0:T(8,128)(2,1)}, u32[]{:S(2)}) %copy-start.1) | copy-done | bytes 458776
  2.5 0.0 copy-start.2
  2.5 0.7 copy-done.2
  3.3 0.0 copy-start.3
  3.3 0.7 copy-done.3
  4.0 74.5 %exchange.1 = (f32[896,4096]{1,0:T(8,128)S(1)}, f32[896,128]{1,0:T(8,128)S(1)}) custom-call(bf16[4,64,3584]{2,1,0:T(8,128)(2,1)S(1)} %bitcast.6, bf16[4,16,64]{2,1,0:T(8,128)(2,1)S(1)} %bitcast.8, bf16[4,16,3584]{2,1,0:T(8,128)(2,1)S(1)} %bitcast.7, bf16[2,2,3584]{2,1,0:T(2,128)(2,1)S(1)} %copy-done.2), custom_call_target="tpu_custom_call" | custom-call | tf_op jit(solution)/shard_map/exchange/pallas_call | solution.py:314
  78.5 7.4 %scale.1 = bf16[896,4096]{1,0:T(8,128)(2,1)} custom-call(f32[896,4096]{1,0:T(8,128)S(1)} %get-tuple-element.7.merged, f32[896,128]{1,0:T(8,128)S(1)} %get-tuple-element.8.scale), custom_call_target="tpu_custom_call" | custom-call | tf_op jit(solution)/shard_map/scale/pallas_call | solution.py:338
Async XLA Ops:
  0.0 1.5 %copy-start = (bf16[2,2,64,3584]{3,2,1,0:T(8,128)(2,1)S(1)}, bf16[2,2,64,3584]{3,2,1,0:T(8,128)(2,1)}, u32[]{:S(2)}) copy-start(bf16[2,2,64,3584]{3,2,1,0:T(8,128)(2,1)} %param.4) | copy-start | bytes 5505028
  1.5 1.0 %copy-start.1 = (bf16[2,2,16,3584]{3,2,1,0:T(8,128)(2,1)S(1)}, bf16[2,2,16,3584]{3,2,1,0:T(8,128)(2,1)}, u32[]{:S(2)}) copy-start(bf16[2,2,16,3584]{3,2,1,0:T(8,128)(2,1)} %param.6) | copy-start | bytes 1376260
  2.5 0.7 copy-start.2
  3.3 0.7 copy-start.3

commit v3 on v2

--- a/solution.py
+++ b/solution.py
@@ -19,7 +19,7 @@
 LROWS = 32
 BROWS = WROWS + LROWS
 RROWS = 32
-LAG1, LAG2 = 2, 2
+LAG1, LAG2, PLAG = 2, 2, 3
 
 
 def packed(load, m):
@@ -35,10 +35,10 @@
             low, high = load(e, 2 * m + 1), load(e, 2 * m - 1)
             group = lax.broadcasted_iota(jnp.int32, low.shape, 1) // 32
             rest.append(jnp.where(group < hole, low, high))
-    last = rest[3]
+    last = rest[3].astype(F32)
     group = lax.broadcasted_iota(jnp.int32, last.shape, 1) // 32
     for k in range(3):
-        full.append(jnp.where(group == hole, pltpu.roll(last, 32 * (k + 1), 1), rest[k]))
+        full.append(jnp.where(group == hole, pltpu.roll(last, 32 * (k + 1), 1).astype(BF16), rest[k]))
     return full
 
 
@@ -46,13 +46,19 @@
     return lax.dot_general(a, b, (((1,), (1,)), ((), ())), preferred_element_type=F32)
 
 
-def offset(i):
-    far = (i + 1) // 2
-    return jnp.where(i % 2 == 1, far, -far)
+SENDS = tuple((d, p) for p in (0, 1) for d in (0, 1, -1, 2, -2)) + tuple((d, p) for p in (0, 1) for d in (3, -3, 4))
+
+
+def arrival(s):
+    far = 2 + (s - 6) // 4
+    dz_near = jnp.where(s % 5 == 0, 0, jnp.where(s % 2 == 1, 1, -1))
+    dz_far = jnp.where(s >= 14, 4, jnp.where(s % 2 == 0, far, -far))
+    other = jnp.where(s < 6, s // 3, jnp.where(s < 14, (s - 6) // 2 % 2, s - 14))
+    return jnp.where(s < 6, dz_near, dz_far), other
 
 
 def exchange_kernel(
-    x_ref, l_ref, r_ref, m_ref, merged, scale_ref, send_buf, rsend, recv, relay, rm, acc, lhs, a_send, l_send, f_send, r_send, recv_sem, l_recv, r_recv
+    x_hbm, l_hbm, r_hbm, m_hbm, merged, scale_ref, x_ref, l_ref, r_ref, m_ref, in_sem, send_buf, rsend, recv, relay, rm, acc, lhs, a_send, l_send, f_send, r_send, recv_sem, l_recv, r_recv
 ):
     t, q = lax.axis_index("tensor"), lax.axis_index("dp")
     xh, y, z = t // 32, (t // 8) % 4, t % 8
@@ -65,7 +71,22 @@
     hole = 3 - row_m
 
     def source(s, parity):
-        return (parity + 2 * (s % 2)) * 8 + (z - offset(s // 2) + 8) % 8
+        dz, other = arrival(s)
+        return (y + (y + parity) % 2 + 2 * other) % 4 * 8 + (z - dz + 8) % 8
+
+    def place(yz):
+        return yz // 16 * 8 + yz % 8
+
+    small_in = [pltpu.make_async_copy(a, b, in_sem.at[4 + k]) for k, (a, b) in enumerate(((l_hbm, l_ref), (r_hbm, r_ref), (m_hbm, m_ref)))]
+
+    def x_in(g):
+        cols = pl.ds(pl.multiple_of(g * (TILES * 128), 128), TILES * 128)
+        return pltpu.make_async_copy(x_hbm.at[:, :, cols], x_ref.at[:, :, cols], in_sem.at[g])
+
+    for a in small_in:
+        a.start()
+    for g in range(4):
+        x_in(g).start()
 
     barrier = pltpu.get_barrier_semaphore()
 
@@ -84,6 +105,8 @@
     def _():
         pl.semaphore_signal(barrier, inc=1, device_id=mirror, device_id_type=MESH)
 
+    for a in small_in:
+        a.wait()
     lanes = lax.broadcasted_iota(jnp.int32, (16, 128), 1)
     ranks = lax.broadcasted_iota(jnp.int32, (16, 128), 0)
     lpack = jnp.zeros((LROWS, 128), F32)
@@ -97,20 +120,32 @@
     @pl.loop(0, 4)
     def _(g):
         base = g * (TILES * 128)
+        x_in(g).wait()
 
         def at(k):
             return pl.ds(pl.multiple_of(base + 128 * k, 128), 128)
 
         for m in range(4):
             d = g * 4 + m
-            for j, tile in enumerate(packed(lambda e, k: x_ref[e, :, at(k)].astype(F32), m)):
-                send_buf[d, j * ROWS : (j + 1) * ROWS, :] = tile.astype(BF16)
+            for j, tile in enumerate(packed(lambda e, k: x_ref[e, :, at(k)], m)):
+                send_buf[d, j * ROWS : (j + 1) * ROWS, :] = tile
             send_buf[d, WROWS:, :] = lpack
-            rt = packed(lambda e, k: r_ref[e, :, at(k)].astype(F32), m)
-            mt = packed(lambda e, k: m_ref[e // 2, :, at(k)].astype(F32)[e % 2 : e % 2 + 1], m)
+
+    mine = q == t // 16
+    for m in range(4):
+
+        @pl.when(jnp.logical_and(mine, row_m == m))
+        def _():
+            base = t % 16 // 4 * (TILES * 128)
+
+            def at(k):
+                return pl.ds(pl.multiple_of(base + 128 * k, 128), 128)
+
+            rt = packed(lambda e, k: r_ref[e, :, at(k)], m)
+            mt = packed(lambda e, k: jnp.broadcast_to(m_ref[e // 2, :, at(k)].astype(F32)[e % 2 : e % 2 + 1], (16, 128)).astype(BF16), m)
             for j in range(TILES):
-                rows = jnp.concatenate([rt[j], jnp.broadcast_to(mt[j], (16, 128))], axis=0)
-                rsend[d, j * RROWS : (j + 1) * RROWS, :] = rows.astype(BF16)
+                rsend[j * RROWS : j * RROWS + 16, :] = rt[j]
+                rsend[j * RROWS + 16 : (j + 1) * RROWS, :] = mt[j]
 
     self_out = jnp.logical_and(src_core == c, dst_core == c).astype(jnp.int32)
     pl.semaphore_wait(barrier, 19 - self_out + inner.astype(jnp.int32))
@@ -120,29 +155,26 @@
             src_ref=src, dst_ref=dst, send_sem=send, recv_sem=recv_s, device_id=dev, device_id_type=MESH
         )
 
-    mine = q == t // 16
-
     def r_copy(k):
-        return copy(rsend.at[t % 16], rm, r_send.at[k], r_recv, (t, (q + 1 + k) % 4))
+        return copy(rsend, rm, r_send.at[k], r_recv, (t, (q + 1 + k) % 4))
 
     @pl.when(mine)
     def _():
         for k in range(3):
             r_copy(k).start()
-        pltpu.make_async_copy(rsend.at[t % 16], rm, r_recv).start()
+        pltpu.make_async_copy(rsend, rm, r_recv).start()
 
     def outgoing(k):
-        yd, zd = 2 * c + (y + k % 2) % 2, (z + offset(k // 2) + 8) % 8
+        dz, p = SENDS[k]
+        yd, zd = 2 * c + (y + p) % 2, (z + dz + 8) % 8
         away = jnp.logical_or(jnp.logical_or(yd != y, zd != z), dst_core != c)
         return yd, zd, away
 
-    @pl.loop(0, 16)
-    def _(k):
+    own = place(y * 8 + z)
+    for k in range(16):
         yd, zd, away = outgoing(k)
-        d = (yd - 2 * c) * 8 + zd
-        s = 2 * (k // 2) + y // 2
         dev = (xh * 32 + yd * 8 + zd, xl * 2 + dst_core)
-        block = send_buf.at[d]
+        block = send_buf.at[(yd - 2 * c) * 8 + zd]
 
         @pl.when(jnp.logical_and(away, edge))
         def _():
@@ -150,7 +182,7 @@
 
         @pl.when(jnp.logical_and(away, inner))
         def _():
-            copy(block, relay.at[s], a_send.at[k], l_recv.at[s], dev).start()
+            copy(block, relay.at[own], a_send.at[k], l_recv.at[own], dev).start()
 
         @pl.when(jnp.logical_and(jnp.logical_not(away), edge))
         def _():
@@ -158,7 +190,7 @@
 
         @pl.when(jnp.logical_and(jnp.logical_not(away), inner))
         def _():
-            pltpu.make_async_copy(block, relay.at[s], l_recv.at[s]).start()
+            pltpu.make_async_copy(block, relay.at[own], l_recv.at[own]).start()
 
     def arrived(slot):
         copy(recv.at[slot], recv.at[slot], f_send.at[0], recv_sem.at[slot], (t, peer)).wait_recv()
@@ -167,15 +199,16 @@
         copy(recv.at[slot], recv.at[slot], f_send.at[k], recv_sem.at[slot], (t, other)).start()
 
     def relayed(s):
-        slot = xh * 32 + source(s, c)
-        return copy(relay.at[s], recv.at[slot], l_send.at[s], recv_sem.at[slot], mirror)
+        yz = source(s, c)
+        slot = xh * 32 + yz
+        return copy(relay.at[place(yz)], recv.at[slot], l_send.at[s], recv_sem.at[slot], mirror)
 
     lane = lax.broadcasted_iota(jnp.int32, (128, 128), 1)
     row = lax.broadcasted_iota(jnp.int32, (128, 128), 0)
     eye = (lane == row).astype(BF16)
 
     def build_lhs():
-        pltpu.make_async_copy(rsend.at[0], rm, r_recv).wait()
+        pltpu.make_async_copy(rsend, rm, r_recv).wait()
         for j in range(TILES):
             r = rm[j * RROWS : j * RROWS + 16, :].astype(F32)
             r8 = jnp.concatenate([r] * 8, axis=0)
@@ -199,8 +232,8 @@
 
     def unit(w):
         stage, who = w // 4, w % 4
-        half = jnp.where(who >= 2, 1 - xl, xl)
-        parity = jnp.where(who % 2 == 1, 1 - c, c)
+        half = jnp.where(who % 2 == 1, 1 - xl, xl)
+        parity = jnp.where(who >= 2, 1 - c, c)
         odd = z % 2
         step = jnp.where(stage == 0, 0, jnp.where(stage == 1, -2, jnp.where(stage == 2, 2, 4)))
         zp = (z - odd + (1 - 2 * odd) * step + 8) % 8
@@ -226,11 +259,12 @@
 
     acc[...] = jnp.zeros_like(acc)
 
-    @pl.loop(0, 21)
+    @pl.loop(0, 23)
     def _(s):
         @pl.when(jnp.logical_and(s < 16, inner))
         def _():
-            copy(relay.at[s], relay.at[s], l_send.at[0], l_recv.at[s], mirror).wait_recv()
+            here = place(source(s, c))
+            copy(relay.at[here], relay.at[here], l_send.at[0], l_recv.at[here], mirror).wait_recv()
             relayed(s).start()
 
         a = s - LAG1
@@ -250,23 +284,23 @@
             arrived(slot)
             forward(slot, 32 + b, peer)
 
-        @pl.when(jnp.logical_and(a >= 1, a < 17))
-        def _():
-            arrived(xl * 32 + source(a - 1, 1 - c))
-
-        @pl.when(jnp.logical_and(b >= 1, b < 17))
-        def _():
-            arrived((1 - xl) * 32 + source(b - 1, 1 - c))
+        @pl.when(jnp.logical_and(a >= PLAG, a < 16 + PLAG))
+        def _():
+            arrived(xl * 32 + source(a - PLAG, 1 - c))
+
+        @pl.when(jnp.logical_and(b >= PLAG, b < 16 + PLAG))
+        def _():
+            arrived((1 - xl) * 32 + source(b - PLAG, 1 - c))
 
         @pl.when(s == 6)
         def _():
             build_lhs()
 
-        @pl.when(s >= 7)
-        def _():
-            @pl.loop(0, jnp.where(jnp.logical_or(s == 17, s == 18), 2, 1))
+        @pl.when(s >= 9)
+        def _():
+            @pl.loop(0, jnp.where(jnp.logical_or(s == 18, s == 20), 2, 1))
             def _(v):
-                unit(jnp.where(s <= 16, s - 7, jnp.where(s <= 18, s - 7 + 2 * v, s - 5)))
+                unit(jnp.where(s <= 19, s - 9 + 3 * v, jnp.where(s == 20, 11 + 2 * v, s - 7)))
 
     for j in range(TILES):
         squares = jnp.sum(acc[j * 128 : (j + 1) * 128, :], axis=1, keepdims=True)
@@ -275,12 +309,14 @@
         for g in range(4):
             scale_ref[pl.ds(starts[j][g], 32), :] = scale[32 * g : 32 * g + 32]
 
+    for k in range(16):
+
+        @pl.when(outgoing(k)[2])
+        def _():
+            copy(send_buf.at[0], relay.at[0], a_send.at[k], l_recv.at[0], mirror).wait_send()
+
     @pl.loop(0, 16)
     def _(k):
-        @pl.when(outgoing(k)[2])
-        def _():
-            copy(send_buf.at[0], relay.at[0], a_send.at[k], l_recv.at[0], mirror).wait_send()
-
         @pl.when(inner)
         def _():
             relayed(k).wait_send()
@@ -295,30 +331,45 @@
             r_copy(k).wait_send()
 
 
-def scale_kernel(merged, scale, out_ref):
-    rows = pl.ds(pl.multiple_of(pl.program_id(0) * 64, 64), 64)
-    s = scale[rows, :]
-
-    @pl.loop(0, T * ROWS // 512)
-    def _(k):
-        for n in range(4):
-            cols = pl.ds(pl.multiple_of(k * 512 + n * 128, 128), 128)
-            out_ref[:, cols] = (merged[rows, cols] * s).astype(BF16)
+def scale_kernel(merged, scale, out_hbm, out_ref, sems):
+    def written(k):
+        rows = pl.ds(k * 128, 128)
+        return pltpu.make_async_copy(out_ref.at[rows], out_hbm.at[rows], sems.at[k])
+
+    for k in range(TILES):
+
+        @pl.loop(0, 8)
+        def _(n):
+            rows = pl.ds(pl.multiple_of(k * 128 + n * 16, 16), 16)
+            s = scale[rows, :]
+            for i in range(T * ROWS // 128):
+                cols = slice(i * 128, i * 128 + 128)
+                out_ref[rows, cols] = (merged[rows, cols] * s).astype(BF16)
+
+        written(k).start()
+    for k in range(TILES):
+        written(k).wait()
 
 
 def shards(base_weight, adapter_left, adapter_right, magnitude):
     x = base_weight.reshape(EPS, ROWS, 3584)
     left = jnp.swapaxes(adapter_left, 2, 3).reshape(EPS, 16, ROWS)
     right = adapter_right.reshape(EPS, 16, 3584)
+    x, left, right, magnitude = (pltpu.with_memory_space_constraint(a, pltpu.HBM) for a in (x, left, right, magnitude))
     vmem = pl.BlockSpec(memory_space=pltpu.VMEM)
     merged, scale = pl.pallas_call(
         exchange_kernel,
         out_shape=(pltpu.VMEM((EPS * SERVE, T * ROWS), F32), pltpu.VMEM((EPS * SERVE, 128), F32)),
-        in_specs=[vmem] * 4,
+        in_specs=[pl.BlockSpec(memory_space=pltpu.HBM)] * 4,
         out_specs=(vmem, vmem),
         scratch_shapes=[
+            pltpu.VMEM((EPS, ROWS, 3584), BF16),
+            pltpu.VMEM((EPS, 16, ROWS), BF16),
+            pltpu.VMEM((EPS, 16, 3584), BF16),
+            pltpu.VMEM((2, 2, 3584), BF16),
+            pltpu.SemaphoreType.DMA((7,)),
             pltpu.VMEM((16, BROWS, 128), BF16),
-            pltpu.VMEM((16, TILES * RROWS, 128), BF16),
+            pltpu.VMEM((TILES * RROWS, 128), BF16),
             pltpu.VMEM((T, BROWS, 128), BF16),
             pltpu.VMEM((16, BROWS, 128), BF16),
             pltpu.VMEM((TILES * RROWS, 128), BF16),
@@ -338,9 +389,9 @@
     out = pl.pallas_call(
         scale_kernel,
         out_shape=jax.ShapeDtypeStruct((EPS * SERVE, T * ROWS), BF16),
-        grid=(EPS * SERVE // 64,),
         in_specs=[vmem, vmem],
-        out_specs=pl.BlockSpec((64, T * ROWS), lambda i: (i, 0)),
+        out_specs=pl.BlockSpec(memory_space=pltpu.HBM),
+        scratch_shapes=[pltpu.VMEM((EPS * SERVE, T * ROWS), BF16), pltpu.SemaphoreType.DMA((TILES,))],
         compiler_params=pltpu.CompilerParams(vmem_limit_bytes=16 * 2**20),
         name="scale",
     )(merged, scale)

time: 87.1 us -> 79.6 us (0.914)
  the two profiles are of different devices: /device:TPU:1 before, /device:TPU:88 now
where the time goes in v3:
time: 79.6 us; the launch traced here: 79.4 us
  Pallas kernels  79.4 us (100%)
    pallas_call x1, Pallas kernels, shards(): pl.pallas_call(exchange_kernel, out_shape=(pltpu.VMEM((EPS * SERVE, T * R...  76.2 us
    pallas_call x1, Pallas kernels, shards(): pl.pallas_call(scale_kernel, out_shape=jax.ShapeDtypeStruct((EPS * SERVE,...  3.24 us

profile of v3, /device:TPU:88, one launch (start us, length us, event | category | flops | bytes accessed | tf_op | source)
XLA Modules:
  0.0 79.4 jit_solution(3380042120466345481)
XLA Ops:
  0.0 76.2 %exchange.1 = (f32[896,4096]{1,0:T(8,128)S(1)}, f32[896,128]{1,0:T(8,128)S(1)}) custom-call(bf16[4,64,3584]{2,1,0:T(8,128)(2,1)} %bitcast.6, bf16[4,16,64]{2,1,0:T(8,128)(2,1)} %bitcast.8, bf16[4,16,3584]{2,1,0:T(8,128)(2,1)} %bitcast.7, bf16[2,2,3584]{2,1,0:T(2,128)(2,1)} %m_hbm.1), custom_call_target="tpu_custom_call" | custom-call | tf_op jit(solution)/shard_map/exchange/pallas_call | solution.py:360
  76.2 3.2 %scale.1 = bf16[896,4096]{1,0:T(8,128)(2,1)} custom-call(f32[896,4096]{1,0:T(8,128)S(1)} %get-tuple-element.7.merged, f32[896,128]{1,0:T(8,128)S(1)} %get-tuple-element.8.scale), custom_call_target="tpu_custom_call" | custom-call | tf_op jit(solution)/shard_map/scale/pallas_call | solution.py:389

commit v4 on v3

--- a/solution.py
+++ b/solution.py
@@ -18,8 +18,10 @@
 WROWS = TILES * ROWS
 LROWS = 32
 BROWS = WROWS + LROWS
-RROWS = 32
-LAG1, LAG2, PLAG = 2, 2, 3
+RROWS = TILES * 16 + 16
+LAG1, LAG2 = 2, 2
+FIRST = 9
+UNITS = (0, 1, 4, 2, 5, 3, 8, 6, 9, 12, 10, 13, 14, 15)
 
 
 def packed(load, m):
@@ -46,15 +48,16 @@
     return lax.dot_general(a, b, (((1,), (1,)), ((), ())), preferred_element_type=F32)
 
 
-SENDS = tuple((d, p) for p in (0, 1) for d in (0, 1, -1, 2, -2)) + tuple((d, p) for p in (0, 1) for d in (3, -3, 4))
+SENDS = tuple((d, p) for d in (0, 1, -1, 2, -2, 3, -3, 4) for p in (0, 1))
 
 
 def arrival(s):
-    far = 2 + (s - 6) // 4
-    dz_near = jnp.where(s % 5 == 0, 0, jnp.where(s % 2 == 1, 1, -1))
-    dz_far = jnp.where(s >= 14, 4, jnp.where(s % 2 == 0, far, -far))
-    other = jnp.where(s < 6, s // 3, jnp.where(s < 14, (s - 6) // 2 % 2, s - 14))
-    return jnp.where(s < 6, dz_near, dz_far), other
+    even = lax.rem(s, 2) == 0
+    far = jnp.where(s >= 10, 3, 2)
+    dz_near = jnp.where(jnp.logical_or(s == 0, s == 5), 0, jnp.where(even, -1, 1))
+    dz_far = jnp.where(s >= 14, 4, jnp.where(even, far, -far))
+    late = jnp.where(s < 6, s >= 3, jnp.where(s < 10, s >= 8, jnp.where(s < 14, s >= 12, s == 15)))
+    return jnp.where(s < 6, dz_near, dz_far), late
 
 
 def exchange_kernel(
@@ -70,12 +73,14 @@
     row_m = t % 4
     hole = 3 - row_m
 
-    def source(s, parity):
-        dz, other = arrival(s)
-        return (y + (y + parity) % 2 + 2 * other) % 4 * 8 + (z - dz + 8) % 8
+    y_rows = [[(y + (y + parity) % 2 + 2 * w) % 4 * 8 for w in range(2)] for parity in (c, 1 - c)]
+
+    def source(s, who):
+        dz, late = arrival(s)
+        return jnp.where(late, y_rows[who][1], y_rows[who][0]) + lax.rem(z - dz + 8, 8)
 
     def place(yz):
-        return yz // 16 * 8 + yz % 8
+        return lax.div(yz, 16) * 8 + lax.rem(yz, 8)
 
     small_in = [pltpu.make_async_copy(a, b, in_sem.at[4 + k]) for k, (a, b) in enumerate(((l_hbm, l_ref), (r_hbm, r_ref), (m_hbm, m_ref)))]
 
@@ -92,13 +97,13 @@
 
     @pl.loop(0, 16)
     def _(s):
-        yz = source(s, c)
+        yz = source(s, 0)
 
         @pl.when(jnp.logical_or(yz != y * 8 + z, src_core != c))
         def _():
             pl.semaphore_signal(barrier, inc=1, device_id=(xh * 32 + yz, xl * 2 + src_core), device_id_type=MESH)
 
-    for other in (nbr, peer, 3 - q):
+    for other in (nbr, peer):
         pl.semaphore_signal(barrier, inc=1, device_id=(t, other), device_id_type=MESH)
 
     @pl.when(inner)
@@ -143,25 +148,29 @@
 
             rt = packed(lambda e, k: r_ref[e, :, at(k)], m)
             mt = packed(lambda e, k: jnp.broadcast_to(m_ref[e // 2, :, at(k)].astype(F32)[e % 2 : e % 2 + 1], (16, 128)).astype(BF16), m)
+            mags = jnp.zeros((16, 128), F32)
             for j in range(TILES):
-                rsend[j * RROWS : j * RROWS + 16, :] = rt[j]
-                rsend[j * RROWS + 16 : (j + 1) * RROWS, :] = mt[j]
+                rsend[j * 16 : j * 16 + 16, :] = rt[j]
+                mags = jnp.where(ranks == j, mt[j].astype(F32), mags)
+            rsend[TILES * 16 :, :] = mags.astype(BF16)
 
     self_out = jnp.logical_and(src_core == c, dst_core == c).astype(jnp.int32)
-    pl.semaphore_wait(barrier, 19 - self_out + inner.astype(jnp.int32))
+    pl.semaphore_wait(barrier, 18 - self_out + inner.astype(jnp.int32))
 
     def copy(src, dst, send, recv_s, dev):
         return pltpu.make_async_remote_copy(
             src_ref=src, dst_ref=dst, send_sem=send, recv_sem=recv_s, device_id=dev, device_id_type=MESH
         )
 
-    def r_copy(k):
-        return copy(rsend, rm, r_send.at[k], r_recv, (t, (q + 1 + k) % 4))
+    second = nbr == t // 16
+
+    def r_copy(src, k):
+        return copy(src, rm, r_send.at[k], r_recv, (t, (peer, nbr)[k]))
 
     @pl.when(mine)
     def _():
-        for k in range(3):
-            r_copy(k).start()
+        for k in range(2):
+            r_copy(rsend, k).start()
         pltpu.make_async_copy(rsend, rm, r_recv).start()
 
     def outgoing(k):
@@ -199,7 +208,7 @@
         copy(recv.at[slot], recv.at[slot], f_send.at[k], recv_sem.at[slot], (t, other)).start()
 
     def relayed(s):
-        yz = source(s, c)
+        yz = source(s, 0)
         slot = xh * 32 + yz
         return copy(relay.at[place(yz)], recv.at[slot], l_send.at[s], recv_sem.at[slot], mirror)
 
@@ -208,9 +217,8 @@
     eye = (lane == row).astype(BF16)
 
     def build_lhs():
-        pltpu.make_async_copy(rsend, rm, r_recv).wait()
         for j in range(TILES):
-            r = rm[j * RROWS : j * RROWS + 16, :].astype(F32)
+            r = rm[j * 16 : j * 16 + 16, :].astype(F32)
             r8 = jnp.concatenate([r] * 8, axis=0)
             e_lane = j if j < 4 else jnp.where(lane // 32 == hole, 3, j - 4)
             rbd = jnp.where((row // 16) % 4 == e_lane, r8, 0.0).astype(BF16)
@@ -239,6 +247,13 @@
         zp = (z - odd + (1 - 2 * odd) * step + 8) % 8
         firsts = [half * 32 + (parity + 2 * h) * 8 + zp for h in range(2)]
         slots = [f + k for f in firsts for k in range(2)]
+
+        @pl.when(who >= 2)
+        def _():
+            @pl.loop(jnp.where(stage == 0, 0, 2 + 4 * stage), jnp.where(stage == 3, 16, 6 + 4 * stage))
+            def _(i):
+                arrived(half * 32 + source(i, 1))
+
         parts = []
         for s in slots:
             lb = recv[s, WROWS:, :].astype(F32)
@@ -263,7 +278,7 @@
     def _(s):
         @pl.when(jnp.logical_and(s < 16, inner))
         def _():
-            here = place(source(s, c))
+            here = place(source(s, 0))
             copy(relay.at[here], relay.at[here], l_send.at[0], l_recv.at[here], mirror).wait_recv()
             relayed(s).start()
 
@@ -271,7 +286,7 @@
 
         @pl.when(jnp.logical_and(a >= 0, a < 16))
         def _():
-            slot = xl * 32 + source(a, c)
+            slot = xl * 32 + source(a, 0)
             arrived(slot)
             forward(slot, a, nbr)
             forward(slot, 16 + a, peer)
@@ -280,32 +295,35 @@
 
         @pl.when(jnp.logical_and(b >= 0, b < 16))
         def _():
-            slot = (1 - xl) * 32 + source(b, c)
+            slot = (1 - xl) * 32 + source(b, 0)
             arrived(slot)
             forward(slot, 32 + b, peer)
 
-        @pl.when(jnp.logical_and(a >= PLAG, a < 16 + PLAG))
-        def _():
-            arrived(xl * 32 + source(a - PLAG, 1 - c))
-
-        @pl.when(jnp.logical_and(b >= PLAG, b < 16 + PLAG))
-        def _():
-            arrived((1 - xl) * 32 + source(b - PLAG, 1 - c))
+        @pl.when(s == 3)
+        def _():
+            pltpu.make_async_copy(rsend, rm, r_recv).wait()
+
+            @pl.when(second)
+            def _():
+                r_copy(rm, 0).start()
 
         @pl.when(s == 6)
         def _():
             build_lhs()
 
-        @pl.when(s >= 9)
-        def _():
-            @pl.loop(0, jnp.where(jnp.logical_or(s == 18, s == 20), 2, 1))
+        @pl.when(s >= FIRST)
+        def _():
+            @pl.loop(0, jnp.where(jnp.logical_or(s == FIRST + 9, s == FIRST + 11), 2, 1))
             def _(v):
-                unit(jnp.where(s <= 19, s - 9 + 3 * v, jnp.where(s == 20, 11 + 2 * v, s - 7)))
-
+                w = jnp.where(s == FIRST + 9, 7, 11)
+                for k, first in enumerate(UNITS):
+                    w = jnp.where(jnp.logical_and(v == 0, s == FIRST + k), first, w)
+                unit(w)
+
+    mags = nt(eye, rm[TILES * 16 :, :])
     for j in range(TILES):
         squares = jnp.sum(acc[j * 128 : (j + 1) * 128, :], axis=1, keepdims=True)
-        mags = nt(eye, rm[j * RROWS + 16 : j * RROWS + 32, :])[:, 0:1]
-        scale = jnp.broadcast_to(mags / jnp.sqrt(squares + 1e-6), (128, 128))
+        scale = jnp.broadcast_to(mags[:, j : j + 1] / jnp.sqrt(squares + 1e-6), (128, 128))
         for g in range(4):
             scale_ref[pl.ds(starts[j][g], 32), :] = scale[32 * g : 32 * g + 32]
 
@@ -327,8 +345,12 @@
 
     @pl.when(mine)
     def _():
-        for k in range(3):
-            r_copy(k).wait_send()
+        for k in range(2):
+            r_copy(rsend, k).wait_send()
+
+    @pl.when(second)
+    def _():
+        r_copy(rm, 0).wait_send()
 
 
 def scale_kernel(merged, scale, out_hbm, out_ref, sems):
@@ -369,16 +391,16 @@
             pltpu.VMEM((2, 2, 3584), BF16),
             pltpu.SemaphoreType.DMA((7,)),
             pltpu.VMEM((16, BROWS, 128), BF16),
-            pltpu.VMEM((TILES * RROWS, 128), BF16),
+            pltpu.VMEM((RROWS, 128), BF16),
             pltpu.VMEM((T, BROWS, 128), BF16),
             pltpu.VMEM((16, BROWS, 128), BF16),
-            pltpu.VMEM((TILES * RROWS, 128), BF16),
+            pltpu.VMEM((RROWS, 128), BF16),
             pltpu.VMEM((EPS * SERVE, 128), F32),
             pltpu.VMEM((TILES, 128, 256), BF16),
             pltpu.SemaphoreType.DMA((16,)),
             pltpu.SemaphoreType.DMA((16,)),
             pltpu.SemaphoreType.DMA((48,)),
-            pltpu.SemaphoreType.DMA((3,)),
+            pltpu.SemaphoreType.DMA((2,)),
             pltpu.SemaphoreType.DMA((T,)),
             pltpu.SemaphoreType.DMA((16,)),
             pltpu.SemaphoreType.DMA,

time: 79.6 us -> 76.1 us (0.956)
  Pallas kernels: 79.4 us -> 75.9 us
    pallas_call x1, Pallas kernels: 76.2 us -> 72.7 us  [shards(): pl.pallas_call(exchange_kernel, out_shape=(pltpu.VMEM((EPS * SERVE, T * R...]
where the time goes in v4:
time: 76.1 us; the launch traced here: 75.9 us
  Pallas kernels  75.9 us (100%)
    pallas_call x1, Pallas kernels, shards(): pl.pallas_call(exchange_kernel, out_shape=(pltpu.VMEM((EPS * SERVE, T * R...  72.7 us
    pallas_call x1, Pallas kernels, shards(): pl.pallas_call(scale_kernel, out_shape=jax.ShapeDtypeStruct((EPS * SERVE,...  3.24 us

profile of v4, /device:TPU:88, one launch (start us, length us, event | category | flops | bytes accessed | tf_op | source)
XLA Modules:
  0.0 75.9 jit_solution(10093105838600905679)
XLA Ops:
  0.0 72.7 %exchange.1 = (f32[896,4096]{1,0:T(8,128)S(1)}, f32[896,128]{1,0:T(8,128)S(1)}) custom-call(bf16[4,64,3584]{2,1,0:T(8,128)(2,1)} %bitcast.6, bf16[4,16,64]{2,1,0:T(8,128)(2,1)} %bitcast.8, bf16[4,16,3584]{2,1,0:T(8,128)(2,1)} %bitcast.7, bf16[2,2,3584]{2,1,0:T(2,128)(2,1)} %m_hbm.1), custom_call_target="tpu_custom_call" | custom-call | tf_op jit(solution)/shard_map/exchange/pallas_call | solution.py:382
  72.7 3.2 %scale.1 = bf16[896,4096]{1,0:T(8,128)(2,1)} custom-call(f32[896,4096]{1,0:T(8,128)S(1)} %get-tuple-element.7.merged, f32[896,128]{1,0:T(8,128)S(1)} %get-tuple-element.8.scale), custom_call_target="tpu_custom_call" | custom-call | tf_op jit(solution)/shard_map/scale/pallas_call | solution.py:411

commit v5 on v4

--- a/solution.py
+++ b/solution.py
@@ -17,11 +17,10 @@
 TILES = 7
 WROWS = TILES * ROWS
 LROWS = 32
-BROWS = WROWS + LROWS
 RROWS = TILES * 16 + 16
 LAG1, LAG2 = 2, 2
 FIRST = 9
-UNITS = (0, 1, 4, 2, 5, 3, 8, 6, 9, 12, 10, 13, 14, 15)
+UNITS = ((0,), (1,), (4,), (2,), (5,), (3,), (8,), (6,), (9, 7), (12, 10, 11), (13, 14), (15,))
 
 
 def packed(load, m):
@@ -61,7 +60,7 @@
 
 
 def exchange_kernel(
-    x_hbm, l_hbm, r_hbm, m_hbm, merged, scale_ref, x_ref, l_ref, r_ref, m_ref, in_sem, send_buf, rsend, recv, relay, rm, acc, lhs, a_send, l_send, f_send, r_send, recv_sem, l_recv, r_recv
+    x_hbm, l_hbm, r_hbm, m_hbm, merged, scale_ref, x_ref, l_ref, r_ref, m_ref, in_sem, send_buf, rsend, recv, relay, rm, acc, lhs, lall, a_send, l_send, f_send, r_send, recv_sem, l_recv, r_recv, g_send, g_recv
 ):
     t, q = lax.axis_index("tensor"), lax.axis_index("dp")
     xh, y, z = t // 32, (t // 8) % 4, t % 8
@@ -103,12 +102,17 @@
         def _():
             pl.semaphore_signal(barrier, inc=1, device_id=(xh * 32 + yz, xl * 2 + src_core), device_id_type=MESH)
 
-    for other in (nbr, peer):
-        pl.semaphore_signal(barrier, inc=1, device_id=(t, other), device_id_type=MESH)
-
-    @pl.when(inner)
-    def _():
-        pl.semaphore_signal(barrier, inc=1, device_id=mirror, device_id_type=MESH)
+    opposite = ((1 - xh) * 32 + y * 8 + z, (1 - xl) * 2 + c)
+
+    def z_partner(k):
+        return (xh * 32 + y * 8 + (z + k) % 8, q)
+
+    def y_partner(k):
+        return (xh * 32 + (y + k) % 4 * 8 + z, q)
+
+    greeted = [(t, nbr), (t, peer), opposite] + [z_partner(k) for k in range(1, 8)] + [y_partner(k) for k in range(1, 4)]
+    for other in greeted:
+        pl.semaphore_signal(barrier, inc=1, device_id=other, device_id_type=MESH)
 
     for a in small_in:
         a.wait()
@@ -120,7 +124,7 @@
         high = (lanes == 64 + e * 16 + ranks).astype(BF16)
         tn = functools.partial(lax.dot_general, dimension_numbers=(((0,), (0,)), ((), ())), preferred_element_type=F32)
         lpack += tn(l_ref[e], low)[:LROWS] + tn(l_ref[e], high)[LROWS:]
-    lpack = lpack.astype(BF16)
+    lall[c, y, z, xh] = jnp.where(c == 0, lpack[:16], lpack[16:]).astype(BF16)
 
     @pl.loop(0, 4)
     def _(g):
@@ -134,7 +138,6 @@
             d = g * 4 + m
             for j, tile in enumerate(packed(lambda e, k: x_ref[e, :, at(k)], m)):
                 send_buf[d, j * ROWS : (j + 1) * ROWS, :] = tile
-            send_buf[d, WROWS:, :] = lpack
 
     mine = q == t // 16
     for m in range(4):
@@ -155,7 +158,7 @@
             rsend[TILES * 16 :, :] = mags.astype(BF16)
 
     self_out = jnp.logical_and(src_core == c, dst_core == c).astype(jnp.int32)
-    pl.semaphore_wait(barrier, 18 - self_out + inner.astype(jnp.int32))
+    pl.semaphore_wait(barrier, 16 + len(greeted) - self_out)
 
     def copy(src, dst, send, recv_s, dev):
         return pltpu.make_async_remote_copy(
@@ -180,7 +183,8 @@
         return yd, zd, away
 
     own = place(y * 8 + z)
-    for k in range(16):
+
+    def send(k):
         yd, zd, away = outgoing(k)
         dev = (xh * 32 + yd * 8 + zd, xl * 2 + dst_core)
         block = send_buf.at[(yd - 2 * c) * 8 + zd]
@@ -200,6 +204,23 @@
         @pl.when(jnp.logical_and(jnp.logical_not(away), inner))
         def _():
             pltpu.make_async_copy(block, relay.at[own], l_recv.at[own]).start()
+
+    def left_copy(ref, k, dev):
+        return copy(ref, ref, g_send.at[k], g_recv.at[k], dev)
+
+    left_x = left_copy(lall.at[c, y, z, xh], 0, opposite)
+    left_z = [left_copy(lall.at[c, y, z], k, z_partner(k)) for k in range(1, 8)]
+    left_y = [left_copy(lall.at[c, y], 7 + k, y_partner(k)) for k in range(1, 4)]
+    left_core = left_copy(lall.at[c], 11, (t, peer))
+
+    left_x.start()
+    for k in range(6):
+        send(k)
+    left_copy(lall.at[c, y, z, 1 - xh], 0, opposite).wait_recv()
+    for m in left_z:
+        m.start()
+    for k in range(6, 10):
+        send(k)
 
     def arrived(slot):
         copy(recv.at[slot], recv.at[slot], f_send.at[0], recv_sem.at[slot], (t, peer)).wait_recv()
@@ -255,8 +276,8 @@
                 arrived(half * 32 + source(i, 1))
 
         parts = []
-        for s in slots:
-            lb = recv[s, WROWS:, :].astype(F32)
+        for h, k in ((0, 0), (0, 1), (1, 0), (1, 1)):
+            lb = jnp.concatenate([lall[n, parity + 2 * h, zp + k, half] for n in range(2)], axis=0).astype(F32)
             parts += [jnp.where(low_half, lb, 0.0), jnp.where(low_half, 0.0, lb)]
         lm = jnp.concatenate(parts, axis=0).astype(BF16)
         for j in range(TILES):
@@ -274,7 +295,7 @@
 
     acc[...] = jnp.zeros_like(acc)
 
-    @pl.loop(0, 23)
+    @pl.loop(0, FIRST + len(UNITS))
     def _(s):
         @pl.when(jnp.logical_and(s < 16, inner))
         def _():
@@ -299,6 +320,25 @@
             arrived(slot)
             forward(slot, 32 + b, peer)
 
+        @pl.when(s == 2)
+        def _():
+            for k in range(1, 8):
+                left_copy(lall.at[c, y, (z - k + 8) % 8], k, z_partner(k)).wait_recv()
+            for m in left_y:
+                m.start()
+            for k in range(10, 16):
+                send(k)
+
+        @pl.when(s == 7)
+        def _():
+            for k in range(1, 4):
+                left_copy(lall.at[c, (y - k + 4) % 4], 7 + k, y_partner(k)).wait_recv()
+            left_core.start()
+
+        @pl.when(s == 8)
+        def _():
+            left_copy(lall.at[1 - c], 11, (t, peer)).wait_recv()
+
         @pl.when(s == 3)
         def _():
             pltpu.make_async_copy(rsend, rm, r_recv).wait()
@@ -313,11 +353,16 @@
 
         @pl.when(s >= FIRST)
         def _():
-            @pl.loop(0, jnp.where(jnp.logical_or(s == FIRST + 9, s == FIRST + 11), 2, 1))
+            count = 1
+            for k, some in enumerate(UNITS):
+                count = jnp.where(s == FIRST + k, len(some), count)
+
+            @pl.loop(0, count)
             def _(v):
-                w = jnp.where(s == FIRST + 9, 7, 11)
-                for k, first in enumerate(UNITS):
-                    w = jnp.where(jnp.logical_and(v == 0, s == FIRST + k), first, w)
+                w = 0
+                for k, some in enumerate(UNITS):
+                    for n, u in enumerate(some):
+                        w = jnp.where(jnp.logical_and(v == n, s == FIRST + k), u, w)
                 unit(w)
 
     mags = nt(eye, rm[TILES * 16 :, :])
@@ -327,6 +372,8 @@
         for g in range(4):
             scale_ref[pl.ds(starts[j][g], 32), :] = scale[32 * g : 32 * g + 32]
 
+    for m in [left_x, left_core] + left_z + left_y:
+        m.wait_send()
     for k in range(16):
 
         @pl.when(outgoing(k)[2])
@@ -390,13 +437,14 @@
             pltpu.VMEM((EPS, 16, 3584), BF16),
             pltpu.VMEM((2, 2, 3584), BF16),
             pltpu.SemaphoreType.DMA((7,)),
-            pltpu.VMEM((16, BROWS, 128), BF16),
+            pltpu.VMEM((16, WROWS, 128), BF16),
             pltpu.VMEM((RROWS, 128), BF16),
-            pltpu.VMEM((T, BROWS, 128), BF16),
-            pltpu.VMEM((16, BROWS, 128), BF16),
+            pltpu.VMEM((T, WROWS, 128), BF16),
+            pltpu.VMEM((16, WROWS, 128), BF16),
             pltpu.VMEM((RROWS, 128), BF16),
             pltpu.VMEM((EPS * SERVE, 128), F32),
             pltpu.VMEM((TILES, 128, 256), BF16),
+            pltpu.VMEM((2, 4, 8, 2, LROWS // 2, 128), BF16),
             pltpu.SemaphoreType.DMA((16,)),
             pltpu.SemaphoreType.DMA((16,)),
             pltpu.SemaphoreType.DMA((48,)),
@@ -404,6 +452,8 @@
             pltpu.SemaphoreType.DMA((T,)),
             pltpu.SemaphoreType.DMA((16,)),
             pltpu.SemaphoreType.DMA,
+            pltpu.SemaphoreType.DMA((12,)),
+            pltpu.SemaphoreType.DMA((12,)),
         ],
         compiler_params=pltpu.CompilerParams(collective_id=0, has_side_effects=True, vmem_limit_bytes=24 * 2**20),
         name="exchange",

time: 76.1 us -> 74.7 us (0.982)
  the two profiles are of different devices: /device:TPU:88 before, /device:TPU:65 now
where the time goes in v5:
time: 74.7 us; the launch traced here: 74.5 us
  Pallas kernels  74.5 us (100%)
    pallas_call x1, Pallas kernels, shards(): pl.pallas_call(exchange_kernel, out_shape=(pltpu.VMEM((EPS * SERVE, T * R...  71.3 us
    pallas_call x1, Pallas kernels, shards(): pl.pallas_call(scale_kernel, out_shape=jax.ShapeDtypeStruct((EPS * SERVE,...  3.24 us

profile of v5, /device:TPU:65, one launch (start us, length us, event | category | flops | bytes accessed | tf_op | source)
XLA Modules:
  0.0 74.5 jit_solution(12110561839942233438)
XLA Ops:
  0.0 71.3 %exchange.1 = (f32[896,4096]{1,0:T(8,128)S(1)}, f32[896,128]{1,0:T(8,128)S(1)}) custom-call(bf16[4,64,3584]{2,1,0:T(8,128)(2,1)} %bitcast.6, bf16[4,16,64]{2,1,0:T(8,128)(2,1)} %bitcast.8, bf16[4,16,3584]{2,1,0:T(8,128)(2,1)} %bitcast.7, bf16[2,2,3584]{2,1,0:T(2,128)(2,1)} %m_hbm.1), custom_call_target="tpu_custom_call" | custom-call | tf_op jit(solution)/shard_map/exchange/pallas_call | solution.py:429
  71.3 3.2 %scale.1 = bf16[896,4096]{1,0:T(8,128)(2,1)} custom-call(f32[896,4096]{1,0:T(8,128)S(1)} %get-tuple-element.7.merged, f32[896,128]{1,0:T(8,128)S(1)} %get-tuple-element.8.scale), custom_call_target="tpu_custom_call" | custom-call | tf_op jit(solution)/shard_map/scale/pallas_call | solution.py:461

commit v6 on v5

--- a/solution.py
+++ b/solution.py
@@ -87,32 +87,32 @@
         cols = pl.ds(pl.multiple_of(g * (TILES * 128), 128), TILES * 128)
         return pltpu.make_async_copy(x_hbm.at[:, :, cols], x_ref.at[:, :, cols], in_sem.at[g])
 
+
+    barrier = pltpu.get_barrier_semaphore()
+
+    for n in range(16):
+        yz = source(15 - n, 0)
+
+        @pl.when(jnp.logical_or(yz != y * 8 + z, src_core != c))
+        def _():
+            pl.semaphore_signal(barrier, inc=1, device_id=(xh * 32 + yz, xl * 2 + src_core), device_id_type=MESH)
+
+    opposite = ((1 - xh) * 32 + y * 8 + z, (1 - xl) * 2 + c)
+
+    def z_partner(k):
+        return (xh * 32 + y * 8 + (z + k) % 8, q)
+
+    def y_partner(k):
+        return (xh * 32 + (y + k) % 4 * 8 + z, q)
+
+    greeted = [z_partner(k) for k in (4, 3, 5, 2, 6, 1, 7)] + [(t, nbr), (t, peer), opposite] + [y_partner(k) for k in range(1, 4)]
+    for other in greeted:
+        pl.semaphore_signal(barrier, inc=1, device_id=other, device_id_type=MESH)
+
     for a in small_in:
         a.start()
     for g in range(4):
         x_in(g).start()
-
-    barrier = pltpu.get_barrier_semaphore()
-
-    @pl.loop(0, 16)
-    def _(s):
-        yz = source(s, 0)
-
-        @pl.when(jnp.logical_or(yz != y * 8 + z, src_core != c))
-        def _():
-            pl.semaphore_signal(barrier, inc=1, device_id=(xh * 32 + yz, xl * 2 + src_core), device_id_type=MESH)
-
-    opposite = ((1 - xh) * 32 + y * 8 + z, (1 - xl) * 2 + c)
-
-    def z_partner(k):
-        return (xh * 32 + y * 8 + (z + k) % 8, q)
-
-    def y_partner(k):
-        return (xh * 32 + (y + k) % 4 * 8 + z, q)
-
-    greeted = [(t, nbr), (t, peer), opposite] + [z_partner(k) for k in range(1, 8)] + [y_partner(k) for k in range(1, 4)]
-    for other in greeted:
-        pl.semaphore_signal(barrier, inc=1, device_id=other, device_id_type=MESH)
 
     for a in small_in:
         a.wait()
@@ -402,21 +402,21 @@
 
 def scale_kernel(merged, scale, out_hbm, out_ref, sems):
     def written(k):
-        rows = pl.ds(k * 128, 128)
+        rows = pl.ds(k * 32, 32)
         return pltpu.make_async_copy(out_ref.at[rows], out_hbm.at[rows], sems.at[k])
 
-    for k in range(TILES):
-
-        @pl.loop(0, 8)
+    for k in range(4 * TILES):
+
+        @pl.loop(0, 2)
         def _(n):
-            rows = pl.ds(pl.multiple_of(k * 128 + n * 16, 16), 16)
+            rows = pl.ds(pl.multiple_of(k * 32 + n * 16, 16), 16)
             s = scale[rows, :]
             for i in range(T * ROWS // 128):
                 cols = slice(i * 128, i * 128 + 128)
                 out_ref[rows, cols] = (merged[rows, cols] * s).astype(BF16)
 
         written(k).start()
-    for k in range(TILES):
+    for k in range(4 * TILES):
         written(k).wait()
 
 
@@ -463,7 +463,7 @@
         out_shape=jax.ShapeDtypeStruct((EPS * SERVE, T * ROWS), BF16),
         in_specs=[vmem, vmem],
         out_specs=pl.BlockSpec(memory_space=pltpu.HBM),
-        scratch_shapes=[pltpu.VMEM((EPS * SERVE, T * ROWS), BF16), pltpu.SemaphoreType.DMA((TILES,))],
+        scratch_shapes=[pltpu.VMEM((EPS * SERVE, T * ROWS), BF16), pltpu.SemaphoreType.DMA((4 * TILES,))],
         compiler_params=pltpu.CompilerParams(vmem_limit_bytes=16 * 2**20),
         name="scale",
     )(merged, scale)

time: 74.7 us -> 72.3 us (0.968)
  the two profiles are of different devices: /device:TPU:65 before, /device:TPU:1 now
where the time goes in v6:
time: 72.3 us; the launch traced here: 72.2 us
  Pallas kernels  72.2 us (100%)
    pallas_call x1, Pallas kernels, shards(): pl.pallas_call(exchange_kernel, out_shape=(pltpu.VMEM((EPS * SERVE, T * R...  68.9 us
    pallas_call x1, Pallas kernels, shards(): pl.pallas_call(scale_kernel, out_shape=jax.ShapeDtypeStruct((EPS * SERVE,...  3.24 us

profile of v6, /device:TPU:1, one launch (start us, length us, event | category | flops | bytes accessed | tf_op | source)
XLA Modules:
  0.0 72.2 jit_solution(12629313161269151874)
XLA Ops:
  0.0 68.9 %exchange.1 = (f32[896,4096]{1,0:T(8,128)S(1)}, f32[896,128]{1,0:T(8,128)S(1)}) custom-call(bf16[4,64,3584]{2,1,0:T(8,128)(2,1)} %bitcast.6, bf16[4,16,64]{2,1,0:T(8,128)(2,1)} %bitcast.8, bf16[4,16,3584]{2,1,0:T(8,128)(2,1)} %bitcast.7, bf16[2,2,3584]{2,1,0:T(2,128)(2,1)} %m_hbm.1), custom_call_target="tpu_custom_call" | custom-call | tf_op jit(solution)/shard_map/exchange/pallas_call | solution.py:429
  68.9 3.2 %scale.1 = bf16[896,4096]{1,0:T(8,128)(2,1)} custom-call(f32[896,4096]{1,0:T(8,128)S(1)} %get-tuple-element.7.merged, f32[896,128]{1,0:T(8,128)S(1)} %get-tuple-element.8.scale), custom_call_target="tpu_custom_call" | custom-call | tf_op jit(solution)/shard_map/scale/pallas_call | solution.py:461

commit v7 on v6

--- a/solution.py
+++ b/solution.py
@@ -18,8 +18,8 @@
 WROWS = TILES * ROWS
 LROWS = 32
 RROWS = TILES * 16 + 16
-LAG1, LAG2 = 2, 2
-FIRST = 9
+LAG1, LAG2 = 2, 3
+FIRST = 10
 UNITS = ((0,), (1,), (4,), (2,), (5,), (3,), (8,), (6,), (9, 7), (12, 10, 11), (13, 14), (15,))
 
 
@@ -219,7 +219,7 @@
     left_copy(lall.at[c, y, z, 1 - xh], 0, opposite).wait_recv()
     for m in left_z:
         m.start()
-    for k in range(6, 10):
+    for k in range(6, 16):
         send(k)
 
     def arrived(slot):
@@ -320,14 +320,12 @@
             arrived(slot)
             forward(slot, 32 + b, peer)
 
-        @pl.when(s == 2)
+        @pl.when(s == 3)
         def _():
             for k in range(1, 8):
                 left_copy(lall.at[c, y, (z - k + 8) % 8], k, z_partner(k)).wait_recv()
             for m in left_y:
                 m.start()
-            for k in range(10, 16):
-                send(k)
 
         @pl.when(s == 7)
         def _():

time: 72.3 us -> 71.7 us (level)
  Pallas kernels: 72.2 us -> 70.9 us
    pallas_call x1, Pallas kernels: 68.9 us -> 67.6 us  [shards(): pl.pallas_call(exchange_kernel, out_shape=(pltpu.VMEM((EPS * SERVE, T * R...]
where the time goes in v7:
time: 71.7 us; the launch traced here: 70.9 us
  Pallas kernels  70.9 us (99%)
    pallas_call x1, Pallas kernels, shards(): pl.pallas_call(exchange_kernel, out_shape=(pltpu.VMEM((EPS * SERVE, T * R...  67.6 us
    pallas_call x1, Pallas kernels, shards(): pl.pallas_call(scale_kernel, out_shape=jax.ShapeDtypeStruct((EPS * SERVE,...  3.24 us

profile of v7, /device:TPU:1, one launch (start us, length us, event | category | flops | bytes accessed | tf_op | source)
XLA Modules:
  0.0 70.9 jit_solution(10300902927517249349)
XLA Ops:
  0.0 67.6 %exchange.1 = (f32[896,4096]{1,0:T(8,128)S(1)}, f32[896,128]{1,0:T(8,128)S(1)}) custom-call(bf16[4,64,3584]{2,1,0:T(8,128)(2,1)} %bitcast.6, bf16[4,16,64]{2,1,0:T(8,128)(2,1)} %bitcast.8, bf16[4,16,3584]{2,1,0:T(8,128)(2,1)} %bitcast.7, bf16[2,2,3584]{2,1,0:T(2,128)(2,1)} %m_hbm.1), custom_call_target="tpu_custom_call" | custom-call | tf_op jit(solution)/shard_map/exchange/pallas_call | solution.py:427
  67.6 3.2 %scale.1 = bf16[896,4096]{1,0:T(8,128)(2,1)} custom-call(f32[896,4096]{1,0:T(8,128)S(1)} %get-tuple-element.7.merged, f32[896,128]{1,0:T(8,128)S(1)} %get-tuple-element.8.scale), custom_call_target="tpu_custom_call" | custom-call | tf_op jit(solution)/shard_map/scale/pallas_call | solution.py:459
